TPU v7x, 32 devices: a whole 2x2x4 slice. The times are simulated.
32 devices in a mesh: gx: 4 (over y, x), gy: 8 (over z, core).
Axes of the slice: x: 2, y: 2, z: 4, core: 2. Of those that a mesh axis runs over, the one named last changes fastest.
Arguments:
- background: float32 [256, 4, 128, 512], P(('gx', 'gy')), may hold values from -6 to 6
- obs_cells: int32 [8, 32, 1024], P('gy', 'gx'), may hold values from 0 to 2303
- obs_counts: int32 [8, 32], P('gy', 'gx'), may hold values from 1 to 1024, as said below
- obs_widths: int32 [8, 32], P('gy', 'gx'), may hold values from 1 to 4
- obs_values: float32 [8, 32, 1024], P('gy', 'gx'), may hold values from -6 to 6
- obs_variances: float32 [8, 32, 1024], P('gy', 'gx'), may hold values from 1 to 16
Outputs:
- analysis: float32 [256, 4, 128, 512], P(('gx', 'gy'))
Inputs may be any that keep to these rules, and one draw needn't show every extreme that they name: `obs_cells`: each is level * 24 * 24 + row * 24 + column of a cell in the patch's surrounding region. `obs_counts`: some patch uses all 1024 slots.
All inputs are finite; a program needn't handle non-finite values.
Results may differ from a plain program's by a relative error of at most 0.0003.
Values sent between devices are 32-bit elements; how exact they have to be, the bound alone decides.
A program may use at most 256 MiB of HBM per device.

v0:
```python
import jax
import jax.numpy as jnp
from jax import lax
from jax.sharding import PartitionSpec as P

PSIDE = 16
HALO = 4
ITERS = 5


def with_halo(x, sides, width, wrap):
    for axis, dim in sides:
        devices, length = (lax.axis_size(axis), x.shape[dim])
        up = [(i, (i + 1) % devices) for i in range(devices if wrap else devices - 1)]
        down = [(j, i) for i, j in up]
        last = lax.slice_in_dim(x, length - width, length, axis=dim)
        leading = lax.slice_in_dim(x, 0, width, axis=dim)
        before = lax.ppermute(last, axis, up)
        after = lax.ppermute(leading, axis, down)
        x = jnp.concatenate([before, x, after], axis=dim)
    return x


def product(former, latter):
    return jnp.einsum("nij,njk->nik", former, latter, precision=lax.Precision.HIGHEST)


def observe_band(
    region, obs_cells, obs_counts, obs_widths, obs_values, obs_variances, core_side, margin
):
    ensemble_members = region.shape[0]
    span_side = core_side + 2 * margin
    lon_width = region.shape[3]
    number = obs_cells.shape[0]
    slots_total = obs_cells.shape[1]
    level_of = obs_cells // (span_side * span_side)
    row_pos = obs_cells // span_side % span_side
    col_pos = obs_cells % span_side
    patch_ids = lax.broadcasted_iota(jnp.int32, obs_cells.shape, 0)
    flat_index = (
        level_of * (span_side * lon_width) + row_pos * lon_width + core_side * patch_ids + col_pos
    )
    flat_region = region.reshape(ensemble_members, region.shape[1] * span_side * lon_width)
    sampled = jnp.take(flat_region, flat_index.reshape(number * slots_total), axis=1)
    sampled = sampled.reshape(ensemble_members, number, slots_total)
    sampled_mean = jnp.mean(sampled, axis=0, keepdims=True)
    observed_spread = sampled - sampled_mean
    innovation = obs_values - sampled_mean[0]
    row_out = jnp.maximum(jnp.maximum(margin - row_pos, row_pos - (margin + core_side - 1)), 0)
    col_out = jnp.maximum(jnp.maximum(margin - col_pos, col_pos - (margin + core_side - 1)), 0)
    distance = jnp.maximum(row_out, col_out)
    slot_ids = lax.broadcasted_iota(jnp.int32, obs_cells.shape, 1)
    usable = (slot_ids < obs_counts[:, None]) & (distance <= obs_widths[:, None])
    relative = distance.astype(jnp.float32) / (obs_widths[:, None] + 1).astype(jnp.float32)
    weights = jnp.where(usable, jnp.exp(-relative * relative) / obs_variances, 0.0)
    scaled_spread = observed_spread * weights[None, :, :]
    pulled = jnp.einsum("kpm,pm->pk", scaled_spread, innovation, precision=lax.Precision.HIGHEST)
    return (scaled_spread, observed_spread, pulled)


def full_gram(scaled_spread, observed_spread):
    return jnp.einsum(
        "swg,zwg->wsz", scaled_spread, observed_spread, precision=lax.Precision.HIGHEST
    )


def transform_of(gram_sum, pulled, sweeps):
    ensemble_members = gram_sum.shape[1]
    identity_m = jnp.eye(ensemble_members, dtype=jnp.float32)
    frobenius = jnp.sqrt(jnp.sum(gram_sum * gram_sum, axis=(1, 2)))
    divisor = ensemble_members - 1.0 + frobenius
    current = (gram_sum + (ensemble_members - 1.0) * identity_m) / divisor[:, None, None]
    inverse_root = jnp.broadcast_to(identity_m, gram_sum.shape)
    for repeat in range(sweeps):
        factor = 1.5 * identity_m - 0.5 * product(inverse_root, current)
        current = product(current, factor)
        inverse_root = product(factor, inverse_root)
    halfway = jnp.einsum("nkj,nj->nk", inverse_root, pulled, precision=lax.Precision.HIGHEST)
    mean_weight = (
        jnp.einsum("nkj,nj->nk", inverse_root, halfway, precision=lax.Precision.HIGHEST)
        / divisor[:, None]
    )
    return (
        jnp.sqrt((ensemble_members - 1.0) / divisor)[:, None, None] * inverse_root
        + mean_weight[:, :, None]
    )


def apply_latitude_band(region, combined, core_side, margin):
    ensemble_members = region.shape[0]
    levels = region.shape[1]
    number = combined.shape[0]
    lon_core = number * core_side
    core_cells = region[:, :, margin : margin + core_side, margin : margin + lon_core]
    patch_centre = jnp.mean(core_cells, axis=0, keepdims=True)
    deviation = core_cells - patch_centre
    inner = levels * core_side
    columns = deviation.reshape(ensemble_members * inner, lon_core).T
    columns = columns.reshape(number, core_side, ensemble_members, inner)
    by_patch = jnp.transpose(columns, (0, 2, 1, 3)).reshape(
        number, ensemble_members, core_side * inner
    )
    mixed = jnp.einsum("pjk,pjx->pkx", combined, by_patch, precision=lax.Precision.HIGHEST)
    mixed = jnp.transpose(mixed.reshape(number, ensemble_members, core_side, inner), (0, 2, 1, 3))
    mixed = mixed.reshape(lon_core, ensemble_members * inner).T.reshape(
        ensemble_members, levels, core_side, lon_core
    )
    return patch_centre + mixed


def shards(background, obs_cells, obs_counts, obs_widths, obs_values, obs_variances):
    members_here = background.shape[0]
    levels = background.shape[1]
    lat_rows = background.shape[2]
    lon_cells = background.shape[3]
    longitude_groups = lax.axis_size("gx")
    groups_y = lax.axis_size("gy")
    lat_local = lat_rows // groups_y
    lon_local = lon_cells // longitude_groups
    arranged = background.reshape(
        members_here, levels, groups_y, lat_local, longitude_groups, lon_local
    )
    arranged = jnp.transpose(arranged, (4, 2, 0, 1, 3, 5)).reshape(
        longitude_groups * groups_y * members_here, levels, lat_local, lon_local
    )
    gathered = lax.all_to_all(arranged, ("gx", "gy"), split_axis=0, concat_axis=0, tiled=True)
    with_rows = with_halo(gathered, (("gy", 2),), HALO, False)
    region = with_halo(with_rows, (("gx", 3),), HALO, True)
    scaled_spread, observed_spread, pulled = observe_band(
        region,
        obs_cells[0],
        obs_counts[0],
        obs_widths[0],
        obs_values[0],
        obs_variances[0],
        PSIDE,
        HALO,
    )
    gram_sum = full_gram(scaled_spread, observed_spread)
    combined = transform_of(gram_sum, pulled, ITERS)
    analysed = apply_latitude_band(region, combined, PSIDE, HALO)
    returned = lax.all_to_all(analysed, ("gx", "gy"), split_axis=0, concat_axis=0, tiled=True)
    returned = returned.reshape(
        longitude_groups, groups_y, members_here, levels, lat_local, lon_local
    )
    result = jnp.transpose(returned, (2, 3, 1, 4, 0, 5)).reshape(
        members_here, levels, lat_rows, lon_cells
    )
    return result


def solution(mesh):
    return jax.shard_map(
        shards,
        mesh=mesh,
        in_specs=(
            P(("gx", "gy"), None, None, None),
            P("gy", "gx", None),
            P("gy", "gx"),
            P("gy", "gx"),
            P("gy", "gx", None),
            P("gy", "gx", None),
        ),
        out_specs=P(("gx", "gy"), None, None, None),
        check_vma=False,
    )
```

profile of v0, /device:TPU:0, one launch (start us, length us, event | category | flops | bytes accessed | tf_op | source)
XLA Modules:
  0.0 765.1 jit_solution(5564560987589936192)
XLA Ops:
  0.0 9.9 %reshape.319 = f32[8,4,8,16,4,128]{5,4,3,2,1,0:T(4,128)} reshape(f32[8,4,128,512]{3,2,1,0:T(8,128)} %param.6) | data formatting | bytes 16777216 | tf_op jit(solution)/shard_map/reshape | solution.py:120
  26.5 183.5 %all-to-all-done = f32[256,4,16,128]{3,2,1,0:T(8,128)} async-done(((f32[256,4,16,128]{3,2,1,0:T(8,128)}), f32[256,4,16,128]{3,2,1,0:T(8,128)}, u32[]{:S(2)}, u32[]{:S(2)}) %all-to-all-start) | async-done | bytes 8388640 | tf_op jit(solution)/shard_map/all_to_all | solution.py:126
  230.2 10.0 %fusion.102 = (f32[256,4,24,4]{3,2,1,0:T(8,128)}, f32[256,4,24,4]{3,2,1,0:T(8,128)}) fusion(f32[256,4,24,128]{3,2,1,0:T(8,128)S(1)} %pad_maximum_fusion.1), kind=kLoop, calls=%fused_computation.166 | loop fusion | bytes 1572864 | tf_op jit(solution)/shard_map/slice | solution.py:16
  240.2 9.1 %copy.32 = f32[256,4,24,4]{0,2,3,1:T(8,128)S(1)} copy(f32[256,4,24,4]{3,2,1,0:T(8,128)} %get-tuple-element.5) | data formatting | bytes 786432 | tf_op jit(solution)/shard_map/slice | solution.py:16
  250.6 9.9 %copy.33 = f32[256,4,24,4]{0,2,3,1:T(8,128)} copy(f32[256,4,24,4]{3,2,1,0:T(8,128)} %get-tuple-element.6) | data formatting | bytes 786432 | tf_op jit(solution)/shard_map/slice | solution.py:17
  262.6 8.7 %broadcast_subtract_fusion = f32[256,4,16,128]{3,2,1,0:T(8,128)} fusion(f32[256,4,16,128]{3,2,1,0:T(8,128)} %all-to-all-done, f32[4,16,128]{2,1,0:T(8,128)S(1)} %broadcast_multiply_fusion.1), kind=kLoop, calls=%fused_computation.17 | loop fusion | flops 2097152 | bytes 16809984 | tf_op jit(solution)/shard_map/sub | solution.py:96
  271.3 9.0 %copy.38 = f32[128,16384]{1,0:T(8,128)} copy(f32[128,16384]{0,1:T(8,128)} %bitcast.189) | data formatting | bytes 16777216 | tf_op jit(solution)/shard_map/transpose | solution.py:98
  280.2 13.1 %reshape.323 = f32[8,16,256,64]{3,2,1,0:T(8,128)} reshape(f32[128,16384]{1,0:T(8,128)} %copy.38) | data formatting | bytes 16777216 | tf_op jit(solution)/shard_map/reshape | solution.py:99
  293.4 12.7 %copy.39 = f32[8,256,16,64]{1,3,2,0:T(8,128)} copy(f32[8,256,16,64]{3,1,2,0:T(8,128)} %bitcast.179) | data formatting | bytes 16777216 | tf_op jit(solution)/shard_map/transpose | solution.py:100
  306.0 10.8 %copy.34 = f32[256,4,24,4]{3,2,1,0:T(8,128)} copy(f32[256,4,24,4]{0,2,3,1:T(8,128)S(1)} %collective-permute-done.2) | data formatting | bytes 786432 | tf_op jit(solution)/shard_map/ppermute | solution.py:18
  316.8 11.6 %copy.35 = f32[256,4,24,4]{3,2,1,0:T(8,128)} copy(f32[256,4,24,4]{0,2,3,1:T(8,128)} %collective-permute-done.3) | data formatting | bytes 786432 | tf_op jit(solution)/shard_map/ppermute | solution.py:19
  328.4 26.5 %pad_maximum_fusion = f32[256,4,24,136]{3,2,1,0:T(8,128)} fusion(f32[256,4,24,4]{3,2,1,0:T(8,128)} %copy.35, f32[256,4,4,128]{3,2,1,0:T(4,128)} %collective-permute-done.1, f32[256,4,16,128]{3,2,1,0:T(8,128)} %all-to-all-done, f32[256,4,4,128]{3,2,1,0:T(4,128)S(1)} %collective-permute-done, f32[256,4,24,4]{3,2,1,0:T(8,128)} %copy.34), kind=kLoop, calls=%fused_computation.1 | loop fusion | flops 13369344 | bytes 26738688 | tf_op jit(solution)/shard_map/concatenate | solution.py:20
  355.0 21.5 %copy.36 = f32[256,4,24,136]{0,3,2,1:T(8,128)} copy(f32[256,4,24,136]{3,2,1,0:T(8,128)} %pad_maximum_fusion) | data formatting | bytes 26738688 | tf_op jit(solution)/shard_map/concatenate | solution.py:20
  376.5 36.2 %gather_fusion = f32[8192,256]{1,0:T(8,128)} fusion(f32[256,13056]{0,1:T(8,128)} %bitcast.177, s32[8192]{0:T(1024)S(1)} %broadcast_clamp_fusion), kind=kCustom, calls=%fused_computation | custom fusion | bytes 16809984 | tf_op jit(solution)/shard_map/jit(_take)/gather | solution.py:44
  417.9 9.2 %copy.37 = f32[256,8,1024]{2,0,1:T(8,128)} copy(f32[256,8,1024]{0,2,1:T(8,128)} %bitcast.178) | data formatting | bytes 16777216 | tf_op jit(solution)/shard_map/jit(_take)/gather | solution.py:44
  427.1 15.2 %multiply_reduce_fusion = (f32[8]{0:T(128)S(1)}, f32[8,256,256]{2,1,0:T(8,128)S(1)}) fusion(f32[256,8,1024]{2,0,1:T(8,128)} %copy.37, f32[8,1024]{1,0:T(8,128)S(1)} %div.115, pred[8,1024]{1,0:T(8,128)(4,1)S(1)} %compare_and_fusion.1, f32[8,1024]{1,0:T(8,128)S(1)} %fusion.70), kind=kOutput, calls=%fused_computation.31 | convolution fusion | flops 6453985280 | bytes 10559520 | tf_op jit(solution)/shard_map/swg,zwg->wsz/dot_general | solution.py:62
  470.1 7.9 %fusion = f32[8,1,256]{2,1,0:T(1,128)S(1)} fusion(f32[256,8,1024]{2,0,1:T(8,128)S(1)} %bitcast.191, f32[8,1024]{1,0:T(8,128)S(1)} %fusion.70, f32[8,1024]{1,0:T(8,128)S(1)} %div.115, pred[8,1024]{1,0:T(8,128)(4,1)S(1)} %compare_and_fusion.1, f32[8,1024,1]{1,0,2:T(8,128)S(1)} %fusion.74), kind=kOutput, calls=%fused_computation.3 | convolution fusion | flops 31457280 | bytes 8503296 | tf_op jit(solution)/shard_map/kpm,pm->pk/dot_general | solution.py:57
  486.5 10.1 %fusion.13 = f32[8,256,1024]{1,2,0:T(8,128)} fusion(f32[8,256,1024]{1,2,0:T(8,128)S(1)} %bitcast.182, f32[8,256,256]{2,1,0:T(8,128)S(1)} %fusion.16, f32[8,256]{1,0:T(8,128)S(1)} %bitcast_divide_fusion, f32[8]{0:T(128)S(1)} %get-tuple-element.19), kind=kOutput, calls=%fused_computation.20 | convolution fusion | flops 6443499520 | bytes 18882592 | tf_op jit(solution)/shard_map/pjk,pjx->pkx/dot_general | solution.py:103
  496.6 12.2 %copy.43 = f32[8,16,256,64]{3,2,1,0:T(8,128)} copy(f32[8,16,256,64]{2,3,1,0:T(8,128)} %bitcast.183) | data formatting | bytes 16777216 | tf_op jit(solution)/shard_map/transpose | solution.py:104
  508.8 12.9 %reshape.326 = f32[128,16384]{1,0:T(8,128)} reshape(f32[8,16,256,64]{3,2,1,0:T(8,128)} %copy.43) | data formatting | bytes 16777216 | tf_op jit(solution)/shard_map/reshape | solution.py:105
  521.6 9.0 %copy.44 = f32[16384,128]{1,0:T(8,128)} copy(f32[16384,128]{0,1:T(8,128)} %bitcast.184) | data formatting | bytes 16777216 | tf_op jit(solution)/shard_map/transpose | solution.py:105
  535.0 207.5 %all_to_all.10 = f32[256,4,16,128]{3,2,1,0:T(8,128)} all-to-all(f32[256,4,16,128]{3,2,1,0:T(8,128)S(1)} %broadcast_add_fusion), channel_id=1, replica_groups=mesh['gx'=4,'gy'=8] {'gx','gy'}, dimensions={0} | all-to-all | bytes 16777216 | tf_op jit(solution)/shard_map/all_to_all | solution.py:142
  742.5 12.1 %copy.45 = f32[8,4,8,16,4,128]{5,4,3,2,1,0:T(4,128)} copy(f32[8,4,8,16,4,128]{5,3,1,0,2,4:T(8,128)} %bitcast.187) | data formatting | bytes 16777216 | tf_op jit(solution)/shard_map/transpose | solution.py:146
  754.6 10.3 %reshape.329 = f32[8,4,128,512]{3,2,1,0:T(8,128)} reshape(f32[8,4,8,16,4,128]{5,4,3,2,1,0:T(4,128)} %copy.45) | data formatting | bytes 16777216 | tf_op jit(solution)/shard_map/reshape | solution.py:146
  (79 shorter events, 85.8 us)
Async XLA Ops:
  17.7 7.5 copy-start
  17.7 8.7 %copy-start.4 = (s32[1,8]{1,0:T(1,128)S(1)}, s32[1,8]{1,0:T(1,128)}, u32[]{:S(2)}) copy-start(s32[1,8]{1,0:T(1,128)} %param.9) | copy-start | bytes 100
  17.7 192.2 %all-to-all-start = ((f32[256,4,16,128]{3,2,1,0:T(8,128)}), f32[256,4,16,128]{3,2,1,0:T(8,128)}, u32[]{:S(2)}, u32[]{:S(2)}) async-start(f32[256,4,16,128]{3,2,1,0:T(8,128)} %bitcast.185), calls=%async_computation | async-start | bytes 16777216 | tf_op jit(solution)/shard_map/all_to_all | solution.py:126
  26.4 193.5 %copy-start.2 = (f32[1,8,1024]{2,1,0:T(8,128)S(1)}, f32[1,8,1024]{2,1,0:T(8,128)}, u32[]{:S(2)}) copy-start(f32[1,8,1024]{2,1,0:T(8,128)} %param.11) | copy-start | bytes 98308
  26.5 193.5 %copy-start.5 = (s32[1,8]{1,0:T(1,128)S(1)}, s32[1,8]{1,0:T(1,128)}, u32[]{:S(2)}) copy-start(s32[1,8]{1,0:T(1,128)} %param.8) | copy-start | bytes 100
  216.5 7.6 collective-permute-start
  218.3 6.4 collective-permute-start.1
  249.3 56.7 %collective-permute-start.2 = (f32[256,4,24,4]{0,2,3,1:T(8,128)S(1)}, f32[256,4,24,4]{0,2,3,1:T(8,128)S(1)}, u32[]{:S(2)}, u32[]{:S(2)}) collective-permute-start(f32[256,4,24,4]{0,2,3,1:T(8,128)S(1)} %copy.32), channel_id=1, source_target_pairs={{0,8},{8,16},{16,24},{24,0},{1,9},{9,17},{17,25},{25,1},{2,10},{10... | collective-permute-start | bytes 1179656 | tf_op jit(solution)/shard_map/ppermute | solution.py:18
  260.5 56.3 %collective-permute-start.3 = (f32[256,4,24,4]{0,2,3,1:T(8,128)}, f32[256,4,24,4]{0,2,3,1:T(8,128)}, u32[]{:S(2)}, u32[]{:S(2)}) collective-permute-start(f32[256,4,24,4]{0,2,3,1:T(8,128)} %copy.33), channel_id=1, source_target_pairs={{8,0},{16,8},{24,16},{0,24},{9,1},{17,9},{25,17},{1,25},{10,2},{18... | collective-permute-start | bytes 1179656 | tf_op jit(solution)/shard_map/ppermute | solution.py:19
  427.1 15.3 %copy-start.1 = (f32[256,256]{1,0:T(8,128)S(1)}, f32[256,256]{1,0:T(8,128)}, u32[]{:S(2)}) copy-start(f32[256,256]{1,0:T(8,128)} %get-tuple-element.25) | copy-start | bytes 786436
  462.8 7.3 slice-start.2
  465.0 5.1 slice-start.3
  467.7 2.3 copy-start.3
  478.0 8.5 %slice-start = ((s8[8388608]{0:T(1024)(128)(4,1)}), s8[4194304]{0:T(1024)(128)(4,1)S(1)}, s32[]{:S(2)}) async-start(s8[8388608]{0:T(1024)(128)(4,1)} %bitcast.180), calls=%async_computation.2 | async-start | bytes 8388608
  480.2 6.3 slice-start.1
where the time goes:
time: 774 us; the launch traced here: 765 us
  local copies, waits for them, and re-layouts  234 us (30%)
  blocking collectives  208 us (27%)
  waiting for transfers between devices  184 us (24%)
  matrix products  69.1 us (9%)
  other arithmetic  55.9 us (7%)
  starting transfers between devices  13.9 us (2%)
    all_to_all x1, blocking collectives, shards(): lax.all_to_all(analysed, ('gx', 'gy'), split_axis=0, concat_axis=0, tiled...  208 us
    all_to_all x1, waiting for transfers between devices, shards(): lax.all_to_all(arranged, ('gx', 'gy'), split_axis=0, concat_axis=0, tiled...  183 us
    gather x2, local copies, waits for them, and re-layouts, observe_band(): jnp.take(flat_region, flat_index.reshape(number * slots_total), axis=1)  45.3 us
    dot_general x14, matrix products, product(): jnp.einsum('nij,njk->nik', former, latter, precision=lax.Precision.HIGHEST)  32.2 us
    concatenate x2, other arithmetic, with_halo(): x = jnp.concatenate([before, x, after], axis=dim)  32.1 us
    slice x3, local copies, waits for them, and re-layouts, with_halo(): last = lax.slice_in_dim(x, length - width, length, axis=dim)  25.6 us
    concatenate x1, local copies, waits for them, and re-layouts, with_halo(): x = jnp.concatenate([before, x, after], axis=dim)  21.5 us
  transfers between devices with their start and end apart: 5, of which 2 were waited for; matrix products, arithmetic and copies ran while one was open for 9% of the time, Pallas kernels for 0%

commit v1 on v0

v1 whole, which is shorter than its diff:
```python
import functools

import jax
import jax.numpy as jnp
from jax import lax
from jax.experimental import pallas as pl
from jax.experimental.pallas import tpu as pltpu
from jax.sharding import PartitionSpec as P

PSIDE = 16
HALO = 4
ITERS = 5
SUB = 8
SPAN = PSIDE + 2 * HALO
HIGHEST = lax.Precision.HIGHEST
VMEM_LIMIT = 48 * 1024 * 1024


def split(x):
    high = x.astype(jnp.bfloat16)
    return high, (x - high.astype(jnp.float32)).astype(jnp.bfloat16)


def dot3(a, b, dims=((1,), (0,))):
    def one(x, y):
        return lax.dot_general(x, y, (dims, ((), ())), preferred_element_type=jnp.float32)

    return one(a[0], b[0]) + (one(a[0], b[1]) + one(a[1], b[0]))


def gram_kernel(first, unroll, core, up, down, left, right, tables, *rest):
    if first:
        gram, pulled, band = rest
    else:
        gram_in, pulled_in, gram, pulled, band = rest
    number = tables.shape[0]
    members = core.shape[2]
    lon = core.shape[1]
    rows = core.shape[0]
    band[0:HALO, SUB : SUB + lon] = up[...]
    band[HALO : HALO + rows, SUB : SUB + lon] = core[...]
    band[HALO + rows : SPAN, SUB : SUB + lon] = down[...]
    band[:, 0:SUB] = left[...]
    band[:, SUB + lon :] = right[...]
    cells = SPAN * SUB
    cell_row = lax.broadcasted_iota(jnp.int32, (cells, SPAN), 0) // SUB
    expand = (cell_row == lax.broadcasted_iota(jnp.int32, (cells, SPAN), 1)).astype(jnp.float32)
    sub = lax.broadcasted_iota(jnp.int32, (cells, 2 * SPAN), 0) % SUB
    lane = lax.broadcasted_iota(jnp.int32, (cells, 2 * SPAN), 1)
    near = lax.broadcasted_iota(jnp.int32, (SPAN, SUB, members), 1) < HALO

    def step(block, carry):
        for inner in range(unroll):
            p = block * unroll + inner
            base = pl.multiple_of(p * PSIDE, SUB)

            def columns(k):
                return band[:, pl.ds(pl.multiple_of(base + k * SUB, SUB), SUB), :]

            pieces = [columns(1), columns(2), jnp.where(near, columns(3), columns(0))]
            table = jnp.dot(
                expand, tables[p], precision=HIGHEST, preferred_element_type=jnp.float32
            )
            spread, scaled, pull = [], [], 0.0
            for g, piece in enumerate(pieces):
                x = piece.reshape(cells, members)
                mean = jnp.mean(x, axis=1, keepdims=True)
                y = x - mean
                w = jnp.sum(jnp.where(lane == g * SUB + sub, table, 0.0), axis=1, keepdims=True)
                u = jnp.sum(
                    jnp.where(lane == SPAN + g * SUB + sub, table, 0.0), axis=1, keepdims=True
                )
                pull = pull + jnp.sum(y * (u - w * mean), axis=0, keepdims=True)
                spread.append(y)
                scaled.append(y * w)
            y = split(jnp.concatenate(spread, axis=0))
            z = split(jnp.concatenate(scaled, axis=0))
            total = dot3(z, y, ((0,), (0,)))
            if first:
                gram[p] = total
                pulled[p] = pull
            else:
                gram[p] = gram_in[p] + total
                pulled[p] = pulled_in[p] + pull
        return carry

    lax.fori_loop(0, number // unroll, step, 0)


def root_kernel(unroll, sweeps, gram, pulled, high_ref, low_ref, mean_ref):
    number = gram.shape[0]
    members = gram.shape[1]
    eye = (
        lax.broadcasted_iota(jnp.int32, (members, members), 0)
        == lax.broadcasted_iota(jnp.int32, (members, members), 1)
    ).astype(jnp.float32)

    def step(block, carry):
        ids = [block * unroll + inner for inner in range(unroll)]
        divisors, currents = [], []
        for p in ids:
            g = gram[p]
            square = jnp.sum(jnp.sum(g * g, axis=0, keepdims=True), axis=1, keepdims=True)
            divisor = members - 1.0 + jnp.sqrt(square)
            divisors.append(divisor)
            currents.append((g + (members - 1.0) * eye) / divisor)
        roots = None
        for repeat in range(sweeps):
            cur = [split(c) for c in currents]
            if repeat == 0:
                factors = [1.5 * eye - 0.5 * c for c in currents]
                fac = [split(f) for f in factors]
                roots = factors
            else:
                old = [split(r) for r in roots]
                factors = [1.5 * eye - 0.5 * dot3(r, c) for r, c in zip(old, cur)]
                fac = [split(f) for f in factors]
                roots = [dot3(f, r) for f, r in zip(fac, old)]
            if repeat < sweeps - 1:
                currents = [dot3(c, f) for c, f in zip(cur, fac)]
        for p, divisor, root in zip(ids, divisors, roots):
            half = jnp.sum(root * pulled[p], axis=1, keepdims=True)
            mean_ref[p] = jnp.sum(root * half, axis=0, keepdims=True) / divisor
            high, low = split(jnp.sqrt((members - 1.0) / divisor) * root)
            high_ref[p] = high
            low_ref[p] = low
        return carry

    lax.fori_loop(0, number // unroll, step, 0)


def apply_kernel(unroll, core, high_ref, low_ref, mean_ref, out):
    number = high_ref.shape[0]
    rows = core.shape[0]
    members = core.shape[2]

    def step(block, carry):
        for inner in range(unroll):
            p = block * unroll + inner
            where = pl.ds(pl.multiple_of(p * PSIDE, PSIDE), PSIDE)
            x = core[:, where, :].reshape(rows * PSIDE, members)
            centre = jnp.mean(x, axis=1, keepdims=True)
            d = x - centre
            shift = centre + jnp.sum(d * mean_ref[p], axis=1, keepdims=True)
            mixed = shift + dot3(split(d), (high_ref[p], low_ref[p]))
            out[:, where, :] = mixed.reshape(rows, PSIDE, members)
        return carry

    lax.fori_loop(0, number // unroll, step, 0)


def vmem(count):
    return [pl.BlockSpec(memory_space=pltpu.VMEM)] * count


def call(kernel, outs, inputs, flops, scratch=(), aliases=None):
    moved = sum(a.size * a.dtype.itemsize for a in (*inputs, *outs))
    return pl.pallas_call(
        kernel,
        out_shape=outs,
        in_specs=vmem(len(inputs)),
        out_specs=vmem(len(outs)),
        scratch_shapes=list(scratch),
        input_output_aliases=aliases or {},
        compiler_params=pltpu.CompilerParams(vmem_limit_bytes=VMEM_LIMIT),
        cost_estimate=pl.CostEstimate(flops=flops, bytes_accessed=moved, transcendentals=0),
    )(*inputs)


def tables_of(obs_cells, obs_counts, obs_widths, obs_values, obs_variances, levels):
    level_of = obs_cells // (SPAN * SPAN)
    row = obs_cells // SPAN % SPAN
    col = obs_cells % SPAN
    row_out = jnp.maximum(jnp.maximum(HALO - row, row - (HALO + PSIDE - 1)), 0)
    col_out = jnp.maximum(jnp.maximum(HALO - col, col - (HALO + PSIDE - 1)), 0)
    distance = jnp.maximum(row_out, col_out)
    slots = lax.broadcasted_iota(jnp.int32, obs_cells.shape, 1)
    usable = (slots < obs_counts[:, None]) & (distance <= obs_widths[:, None])
    relative = distance.astype(jnp.float32) / (obs_widths[:, None] + 1).astype(jnp.float32)
    weights = jnp.where(usable, jnp.exp(-relative * relative) / obs_variances, 0.0)
    place = jnp.where(
        col < HALO,
        PSIDE + HALO + col,
        col - HALO,
    )
    line = level_of * SPAN + row
    hot_line = (line[:, :, None] == jnp.arange(levels * SPAN)).astype(jnp.float32)
    hot_place = place[:, :, None] == jnp.arange(SPAN)
    sums = jnp.concatenate(
        [
            jnp.where(hot_place, weights[:, :, None], 0.0),
            jnp.where(hot_place, (weights * obs_values)[:, :, None], 0.0),
        ],
        axis=2,
    )
    table = jnp.einsum("psl,psg->plg", hot_line, sums, precision=HIGHEST)
    return table.reshape(table.shape[0], levels, SPAN, 2 * SPAN)


def shift(x, axis, step, wrap):
    n = lax.axis_size(axis)
    pairs = [(i, (i + step) % n) for i in range(n) if wrap or 0 <= i + step < n]
    return lax.ppermute(x, axis, pairs)


def shards(background, obs_cells, obs_counts, obs_widths, obs_values, obs_variances):
    here, levels, lat_rows, lon_cells = background.shape
    nx = lax.axis_size("gx")
    ny = lax.axis_size("gy")
    lat = lat_rows // ny
    lon = lon_cells // nx
    members = nx * ny * here
    number = lon // PSIDE
    tables = tables_of(
        obs_cells[0], obs_counts[0], obs_widths[0], obs_values[0], obs_variances[0], levels
    )
    cores, state = [], ()
    for level in range(levels):
        arranged = background[:, level].reshape(here, ny, lat, nx, lon)
        arranged = jnp.transpose(arranged, (3, 1, 0, 2, 4)).reshape(members, lat, lon)
        gathered = lax.all_to_all(arranged, ("gx", "gy"), split_axis=0, concat_axis=0, tiled=True)
        core = jnp.transpose(gathered, (1, 2, 0))
        cores.append(core)
        up = shift(core[lat - HALO :], "gy", 1, False)
        down = shift(core[:HALO], "gy", -1, False)

        def edge(side):
            return jnp.concatenate([up[:, side], core[:, side], down[:, side]], axis=0)

        left = shift(edge(slice(lon - SUB, lon)), "gx", 1, True)
        right = shift(edge(slice(0, SUB)), "gx", -1, True)
        inputs = (core, up, down, left, right, tables[:, level], *state)
        state = call(
            functools.partial(gram_kernel, level == 0, 2),
            (
                jax.ShapeDtypeStruct((number, members, members), jnp.float32),
                jax.ShapeDtypeStruct((number, 1, members), jnp.float32),
            ),
            inputs,
            6 * number * members * members * SPAN * SPAN,
            scratch=[pltpu.VMEM((SPAN, lon + 2 * SUB, members), jnp.float32)],
            aliases=None if level == 0 else {6: 0, 7: 1},
        )
    square = jax.ShapeDtypeStruct((number, members, members), jnp.bfloat16)
    transform = call(
        functools.partial(root_kernel, 2, ITERS),
        (square, square, jax.ShapeDtypeStruct((number, 1, members), jnp.float32)),
        state,
        72 * number * members**3,
    )
    results = []
    for level in range(levels):
        (mixed,) = call(
            functools.partial(apply_kernel, 2),
            (jax.ShapeDtypeStruct((lat, lon, members), jnp.float32),),
            (cores[level], *transform),
            6 * lat * lon * members * members,
        )
        mixed = jnp.transpose(mixed, (2, 0, 1))
        returned = lax.all_to_all(mixed, ("gx", "gy"), split_axis=0, concat_axis=0, tiled=True)
        returned = returned.reshape(nx, ny, here, lat, lon)
        results.append(jnp.transpose(returned, (2, 1, 3, 0, 4)).reshape(here, lat_rows, lon_cells))
    return jnp.stack(results, axis=1)


def solution(mesh):
    return jax.shard_map(
        shards,
        mesh=mesh,
        in_specs=(
            P(("gx", "gy"), None, None, None),
            P("gy", "gx", None),
            P("gy", "gx"),
            P("gy", "gx"),
            P("gy", "gx", None),
            P("gy", "gx", None),
        ),
        out_specs=P(("gx", "gy"), None, None, None),
        check_vma=False,
    )
```

time: 774 us -> 543 us (0.70)
  blocking collectives: 208 us -> 0 us
  waiting for transfers between devices: 184 us -> 318 us
  local copies, waits for them, and re-layouts: 234 us -> 102 us
  matrix products: 69.1 us -> 1.76 us
  Pallas kernels: 0 us -> 58.6 us
  other arithmetic: 55.9 us -> 3.79 us
  starting transfers between devices: 13.9 us -> 56.7 us
    all_to_all x1 -> x0, blocking collectives: 208 us -> none  [shards(): lax.all_to_all(analysed, ('gx', 'gy'), split_axis=0, concat_axis=0, tiled...]
    all_to_all x0 -> x4, waiting for transfers between devices: none -> 154 us  [shards(): lax.all_to_all(mixed, ('gx', 'gy'), split_axis=0, concat_axis=0, tiled=True)]
    dot_general x19 -> x1, matrix products: 69.1 us -> 1.76 us  [tables_of(): table = jnp.einsum('psl,psg->plg', hot_line, sums, precision=HIGHEST)]
    pallas_call x0 -> x9, Pallas kernels: none -> 58.6 us  [call(): pl.pallas_call(kernel, out_shape=outs, in_specs=vmem(len(inputs)), out_sp...]
    reshape x4 -> x0, local copies, waits for them, and re-layouts: 46.1 us -> none  [the longest x1 13.1 us: apply_latitude_band(): columns = columns.reshape(number, core_side, ensemble_members, inner)]
    gather x2 -> x0, local copies, waits for them, and re-layouts: 45.3 us -> none  [observe_band(): jnp.take(flat_region, flat_index.reshape(number * slots_total), axis=1)]
    concatenate x2 -> x8, other arithmetic: 32.1 us -> 0.12 us  [edge(): return jnp.concatenate([up[:, side], core[:, side], down[:, side]], axis=0)]
    all_to_all x1 -> x4, waiting for transfers between devices: 183 us -> 157 us  [shards(): lax.all_to_all(arranged, ('gx', 'gy'), split_axis=0, concat_axis=0, tiled...]
  transfers between devices with their start and end apart: 5 -> 24, of which waited for: 2 -> 12; matrix products, arithmetic and copies ran while one was open for 9% -> 13% of each run, Pallas kernels for 0% -> 6%
where the time goes in v1:
time: 543 us; the launch traced here: 541 us
  waiting for transfers between devices  318 us (59%)
  local copies, waits for them, and re-layouts  102 us (19%)
  Pallas kernels  58.6 us (11%)
  starting transfers between devices  56.7 us (10%)
    all_to_all x4, waiting for transfers between devices, shards(): lax.all_to_all(arranged, ('gx', 'gy'), split_axis=0, concat_axis=0, tiled...  157 us
    all_to_all x4, waiting for transfers between devices, shards(): lax.all_to_all(mixed, ('gx', 'gy'), split_axis=0, concat_axis=0, tiled=True)  154 us
    pallas_call x9, Pallas kernels, call(): pl.pallas_call(kernel, out_shape=outs, in_specs=vmem(len(inputs)), out_sp...  58.6 us
    ppermute x16, starting transfers between devices, shift(): return lax.ppermute(x, axis, pairs)  26.2 us
    all_to_all x4, starting transfers between devices, shards(): lax.all_to_all(arranged, ('gx', 'gy'), split_axis=0, concat_axis=0, tiled...  17 us
    another operation x5, local copies, waits for them, and re-layouts, shards(): return jnp.stack(results, axis=1)  16.8 us
    transpose x4, local copies, waits for them, and re-layouts, shards(): jnp.transpose(returned, (2, 1, 3, 0, 4)).reshape(here, lat_rows, lon_cells)  15.4 us
    all_to_all x4, starting transfers between devices, shards(): lax.all_to_all(mixed, ('gx', 'gy'), split_axis=0, concat_axis=0, tiled=True)  13.4 us
  transfers between devices with their start and end apart: 24, of which 12 were waited for; matrix products, arithmetic and copies ran while one was open for 13% of the time, Pallas kernels for 6%

profile of v1, /device:TPU:0, one launch (start us, length us, event | category | flops | bytes accessed | tf_op | source)
XLA Modules:
  0.0 541.4 jit_solution(5359119905765906629)
XLA Ops:
  0.0 7.3 %fusion.20 = (f32[8,1,128,512]{3,2,1,0:T(8,128)}, f32[8,1,128,512]{3,2,1,0:T(8,128)}, f32[8,1,128,512]{3,2,1,0:T(8,128)}, f32[8,1,128,512]{3,2,1,0:T(8,128)}) fusion(f32[8,4,128,512]{3,2,1,0:T(8,128)} %param.6), kind=kLoop, calls=%fused_computation.48 | loop fusion | bytes 16777216 | tf_op jit(solution)/shard_map/slice | solution.py:219
  10.8 7.3 %all-to-all-start = ((f32[256,16,128]{2,1,0:T(8,128)}), f32[256,16,128]{2,1,0:T(8,128)S(1)}, u32[]{:S(2)}, u32[]{:S(2)}) async-start(f32[256,16,128]{2,1,0:T(8,128)} %bitcast.129), calls=%async_computation | async-start | bytes 4194304 | tf_op jit(solution)/shard_map/all_to_all | solution.py:221
  24.3 43.9 %all-to-all-done = f32[256,16,128]{2,1,0:T(8,128)S(1)} async-done(((f32[256,16,128]{2,1,0:T(8,128)}), f32[256,16,128]{2,1,0:T(8,128)S(1)}, u32[]{:S(2)}, u32[]{:S(2)}) %all-to-all-start) | async-done | bytes 2097184 | tf_op jit(solution)/shard_map/all_to_all | solution.py:221
  69.5 3.5 all-to-all-start.1
  76.7 46.4 %all-to-all-done.1 = f32[256,16,128]{2,1,0:T(8,128)} async-done(((f32[256,16,128]{2,1,0:T(8,128)}), f32[256,16,128]{2,1,0:T(8,128)}, u32[]{:S(2)}, u32[]{:S(2)}) %all-to-all-start.1) | async-done | bytes 2097184 | tf_op jit(solution)/shard_map/all_to_all | solution.py:221
  131.9 43.9 %all-to-all-done.3 = f32[256,16,128]{2,1,0:T(8,128)S(1)} async-done(((f32[256,16,128]{2,1,0:T(8,128)}), f32[256,16,128]{2,1,0:T(8,128)S(1)}, u32[]{:S(2)}, u32[]{:S(2)}) %all-to-all-start.3) | async-done | bytes 2097184 | tf_op jit(solution)/shard_map/all_to_all | solution.py:221
  189.8 3.7 copy.66
  199.1 3.8 collective-permute-start.12
  208.5 22.4 %all-to-all-done.2 = f32[256,16,128]{2,1,0:T(8,128)} async-done(((f32[256,16,128]{2,1,0:T(8,128)}), f32[256,16,128]{2,1,0:T(8,128)}, u32[]{:S(2)}, u32[]{:S(2)}) %all-to-all-start.2) | async-done | bytes 2097184 | tf_op jit(solution)/shard_map/all_to_all | solution.py:221
  253.1 3.5 collective-permute-done.15.right
  258.0 7.9 %shard_map.64 = (f32[8,256,256]{2,1,0:T(8,128)S(1)}, f32[8,1,256]{2,1,0:T(1,128)S(1)}) custom-call(f32[16,128,256]{2,1,0:T(8,128)S(1)} %bitcast.113, f32[4,128,256]{2,1,0:T(8,128)} %collective-permute-done.12.up, f32[4,128,256]{2,1,0:T(8,128)} %collective-permute-done.13.down, f32[24,8,256]{2,1,0:T(8,128)S(1)} %collective-permute-done.14.left, ...), custom_call_target="tpu_custom_call" | custom-call | flops 1811939328 | bytes 5681152 | tf_op jit(solution)/shard_map/pallas_call | solution.py:158
  269.3 7.9 %shard_map.65 = (f32[8,256,256]{2,1,0:T(8,128)S(1)}, f32[8,1,256]{2,1,0:T(1,128)S(1)}) custom-call(f32[16,128,256]{2,1,0:T(8,128)S(1)} %bitcast.117, f32[4,128,256]{2,1,0:T(8,128)S(1)} %collective-permute-done.8.up, f32[4,128,256]{2,1,0:T(8,128)} %collective-permute-done.9.down, ...), custom_call_target="tpu_custom_call", output_to_operand_aliasing={{0}: (6, {}), {1}: (7, {})} | custom-call | flops 1811939328 | bytes 7786496 | tf_op jit(solution)/shard_map/pallas_call | solution.py:158
  277.7 6.7 %shard_map.66 = (f32[8,256,256]{2,1,0:T(8,128)S(1)}, f32[8,1,256]{2,1,0:T(1,128)S(1)}) custom-call(f32[16,128,256]{2,1,0:T(8,128)S(1)} %bitcast.121, f32[4,128,256]{2,1,0:T(8,128)S(1)} %collective-permute-done.4.up, f32[4,128,256]{2,1,0:T(8,128)S(1)} %collective-permute-done.5.down, ...), custom_call_target="tpu_custom_call", output_to_operand_aliasing={{0}: (6, {}), {1}: (7, {})} | custom-call | flops 1811939328 | bytes 7786496 | tf_op jit(solution)/shard_map/pallas_call | solution.py:158
  284.5 6.7 %shard_map.67 = (f32[8,256,256]{2,1,0:T(8,128)S(1)}, f32[8,1,256]{2,1,0:T(1,128)S(1)}) custom-call(f32[16,128,256]{2,1,0:T(8,128)S(1)} %bitcast.108, f32[4,128,256]{2,1,0:T(8,128)S(1)} %collective-permute-done.up, f32[4,128,256]{2,1,0:T(8,128)S(1)} %collective-permute-done.1.down, ...), custom_call_target="tpu_custom_call", output_to_operand_aliasing={{0}: (6, {}), {1}: (7, {})} | custom-call | flops 1811939328 | bytes 7786496 | tf_op jit(solution)/shard_map/pallas_call | solution.py:158
  291.2 15.4 %shard_map.68 = (bf16[8,256,256]{2,1,0:T(8,128)(2,1)S(1)}, bf16[8,256,256]{2,1,0:T(8,128)(2,1)S(1)}, f32[8,1,256]{2,1,0:T(1,128)S(1)}) custom-call(f32[8,256,256]{2,1,0:T(8,128)S(1)} %get-tuple-element.22.gram, f32[8,1,256]{2,1,0:T(1,128)S(1)} %get-tuple-element.23.pulled), custom_call_target="tpu_custom_call" | custom-call | flops 9663676416 | bytes 4210688 | tf_op jit(solution)/shard_map/pallas_call | solution.py:158
  314.5 3.5 all-to-all-start.5
  325.9 42.1 %all-to-all-done.5 = f32[256,16,128]{2,1,0:T(8,128)} async-done(((f32[256,16,128]{2,1,0:T(8,128)}), f32[256,16,128]{2,1,0:T(8,128)}, u32[]{:S(2)}, u32[]{:S(2)}) %all-to-all-start.5) | async-done | bytes 2097184 | tf_op jit(solution)/shard_map/all_to_all | solution.py:260
  379.4 42.1 %all-to-all-done.4 = f32[256,16,128]{2,1,0:T(8,128)} async-done(((f32[256,16,128]{2,1,0:T(8,128)}), f32[256,16,128]{2,1,0:T(8,128)}, u32[]{:S(2)}, u32[]{:S(2)}) %all-to-all-start.4) | async-done | bytes 2097184 | tf_op jit(solution)/shard_map/all_to_all | solution.py:260
  432.9 42.1 %all-to-all-done.6 = f32[256,16,128]{2,1,0:T(8,128)} async-done(((f32[256,16,128]{2,1,0:T(8,128)}), f32[256,16,128]{2,1,0:T(8,128)}, u32[]{:S(2)}, u32[]{:S(2)}) %all-to-all-start.6) | async-done | bytes 2097184 | tf_op jit(solution)/shard_map/all_to_all | solution.py:260
  478.0 4.3 copy.72
  485.3 4.3 copy.70
  492.6 4.3 copy.74
  500.0 27.8 %all-to-all-done.7 = f32[256,16,128]{2,1,0:T(8,128)S(1)} async-done(((f32[256,16,128]{2,1,0:T(8,128)}), f32[256,16,128]{2,1,0:T(8,128)S(1)}, u32[]{:S(2)}, u32[]{:S(2)}) %all-to-all-start.7) | async-done | bytes 2097184 | tf_op jit(solution)/shard_map/all_to_all | solution.py:260
  537.0 4.4 copy.77
  (140 shorter events, 135.5 us)
Async XLA Ops:
  10.8 57.4 %all-to-all-start = ((f32[256,16,128]{2,1,0:T(8,128)}), f32[256,16,128]{2,1,0:T(8,128)S(1)}, u32[]{:S(2)}, u32[]{:S(2)}) async-start(f32[256,16,128]{2,1,0:T(8,128)} %bitcast.129), calls=%async_computation | async-start | bytes 4194304 | tf_op jit(solution)/shard_map/all_to_all | solution.py:221
  69.5 53.5 %all-to-all-start.1 = ((f32[256,16,128]{2,1,0:T(8,128)}), f32[256,16,128]{2,1,0:T(8,128)}, u32[]{:S(2)}, u32[]{:S(2)}) async-start(f32[256,16,128]{2,1,0:T(8,128)} %bitcast.128), calls=%async_computation.1 | async-start | bytes 4194304 | tf_op jit(solution)/shard_map/all_to_all | solution.py:221
  123.0 52.8 %all-to-all-start.3 = ((f32[256,16,128]{2,1,0:T(8,128)}), f32[256,16,128]{2,1,0:T(8,128)S(1)}, u32[]{:S(2)}, u32[]{:S(2)}) async-start(f32[256,16,128]{2,1,0:T(8,128)} %bitcast.127), calls=%async_computation.3 | async-start | bytes 4194304 | tf_op jit(solution)/shard_map/all_to_all | solution.py:221
  177.3 53.6 %all-to-all-start.2 = ((f32[256,16,128]{2,1,0:T(8,128)}), f32[256,16,128]{2,1,0:T(8,128)}, u32[]{:S(2)}, u32[]{:S(2)}) async-start(f32[256,16,128]{2,1,0:T(8,128)} %bitcast.18), calls=%async_computation.2 | async-start | bytes 4194304 | tf_op jit(solution)/shard_map/all_to_all | solution.py:221
  186.6 49.7 %collective-permute-start.13 = (f32[4,128,256]{2,1,0:T(8,128)}, f32[4,128,256]{2,1,0:T(8,128)}, u32[]{:S(2)}, u32[]{:S(2)}) collective-permute-start(f32[4,128,256]{2,1,0:T(8,128)} %get-tuple-element.35), channel_id=1, source_target_pairs={{1,0},{2,1},{3,2},{4,3},{5,4},{6,5},{7,6},{9,8},{10,9},{11,10},{12... | collective-permute-start | bytes 1572872 | tf_op jit(solution)/shard_map/ppermute | solution.py:203
  199.1 39.8 %collective-permute-start.12 = (f32[4,128,256]{2,1,0:T(8,128)}, f32[4,128,256]{2,1,0:T(8,128)}, u32[]{:S(2)}, u32[]{:S(2)}) collective-permute-start(f32[4,128,256]{2,1,0:T(8,128)} %get-tuple-element.36), channel_id=1, source_target_pairs={{0,1},{1,2},{2,3},{3,4},{4,5},{5,6},{6,7},{8,9},{9,10},{10,11},{11... | collective-permute-start | bytes 1572872 | tf_op jit(solution)/shard_map/ppermute | solution.py:203
  202.9 38.1 %collective-permute-start.1 = (f32[4,128,256]{2,1,0:T(8,128)}, f32[4,128,256]{2,1,0:T(8,128)S(1)}, u32[]{:S(2)}, u32[]{:S(2)}) collective-permute-start(f32[4,128,256]{2,1,0:T(8,128)} %get-tuple-element.47), channel_id=1, source_target_pairs={{1,0},{2,1},{3,2},{4,3},{5,4},{6,5},{7,6},{9,8},{10,9},{11,10},{12... | collective-permute-start | bytes 1572872 | tf_op jit(solution)/shard_map/ppermute | solution.py:203
  204.2 39.9 %collective-permute-start = (f32[4,128,256]{2,1,0:T(8,128)}, f32[4,128,256]{2,1,0:T(8,128)S(1)}, u32[]{:S(2)}, u32[]{:S(2)}) collective-permute-start(f32[4,128,256]{2,1,0:T(8,128)} %get-tuple-element.48), channel_id=1, source_target_pairs={{0,1},{1,2},{2,3},{3,4},{4,5},{5,6},{6,7},{8,9},{9,10},{10,11},{11... | collective-permute-start | bytes 1572872 | tf_op jit(solution)/shard_map/ppermute | solution.py:203
  207.2 38.2 %collective-permute-start.9 = (f32[4,128,256]{2,1,0:T(8,128)}, f32[4,128,256]{2,1,0:T(8,128)}, u32[]{:S(2)}, u32[]{:S(2)}) collective-permute-start(f32[4,128,256]{2,1,0:T(8,128)} %get-tuple-element.39), channel_id=1, source_target_pairs={{1,0},{2,1},{3,2},{4,3},{5,4},{6,5},{7,6},{9,8},{10,9},{11,10},{12... | collective-permute-start | bytes 1572872 | tf_op jit(solution)/shard_map/ppermute | solution.py:203
  236.3 11.7 %collective-permute-start.8 = (f32[4,128,256]{2,1,0:T(8,128)S(1)}, f32[4,128,256]{2,1,0:T(8,128)S(1)}, u32[]{:S(2)}, u32[]{:S(2)}) collective-permute-start(f32[4,128,256]{2,1,0:T(8,128)S(1)} %copy-done.19), channel_id=1, source_target_pairs={{0,1},{1,2},{2,3},{3,4},{4,5},{5,6},{6,7},{8,9},{9,10},{10,11},{11... | collective-permute-start | bytes 1572872 | tf_op jit(solution)/shard_map/ppermute | solution.py:203
  238.9 9.6 %collective-permute-start.5 = (f32[4,128,256]{2,1,0:T(8,128)S(1)}, f32[4,128,256]{2,1,0:T(8,128)S(1)}, u32[]{:S(2)}, u32[]{:S(2)}) collective-permute-start(f32[4,128,256]{2,1,0:T(8,128)S(1)} %get-tuple-element.43), channel_id=1, source_target_pairs={{1,0},{2,1},{3,2},{4,3},{5,4},{6,5},{7,6},{9,8},{10,9},{11,10},{12... | collective-permute-start | bytes 1572872 | tf_op jit(solution)/shard_map/ppermute | solution.py:203
  241.0 9.9 %collective-permute-start.4 = (f32[4,128,256]{2,1,0:T(8,128)S(1)}, f32[4,128,256]{2,1,0:T(8,128)S(1)}, u32[]{:S(2)}, u32[]{:S(2)}) collective-permute-start(f32[4,128,256]{2,1,0:T(8,128)S(1)} %get-tuple-element.44), channel_id=1, source_target_pairs={{0,1},{1,2},{2,3},{3,4},{4,5},{5,6},{6,7},{8,9},{9,10},{10,11},{11... | collective-permute-start | bytes 1572872 | tf_op jit(solution)/shard_map/ppermute | solution.py:203
  244.1 8.5 %collective-permute-start.14 = (f32[24,8,256]{2,1,0:T(8,128)S(1)}, f32[24,8,256]{2,1,0:T(8,128)S(1)}, u32[]{:S(2)}, u32[]{:S(2)}) collective-permute-start(f32[24,8,256]{2,1,0:T(8,128)S(1)} %pad_maximum_fusion.7), channel_id=1, source_target_pairs={{0,8},{8,16},{16,24},{24,0},{1,9},{9,17},{17,25},{25,1},{2,10},{10... | collective-permute-start | bytes 589832 | tf_op jit(solution)/shard_map/ppermute | solution.py:203
  245.4 11.2 %collective-permute-start.15 = (f32[24,8,256]{2,1,0:T(8,128)S(1)}, f32[24,8,256]{2,1,0:T(8,128)S(1)}, u32[]{:S(2)}, u32[]{:S(2)}) collective-permute-start(f32[24,8,256]{2,1,0:T(8,128)S(1)} %pad_maximum_fusion.8), channel_id=1, source_target_pairs={{0,24},{8,0},{16,8},{24,16},{1,25},{9,1},{17,9},{25,17},{2,26},{10... | collective-permute-start | bytes 589832 | tf_op jit(solution)/shard_map/ppermute | solution.py:203
  248.0 36.4 %collective-permute-start.2 = (f32[24,8,256]{2,1,0:T(8,128)S(1)}, f32[24,8,256]{2,1,0:T(8,128)S(1)}, u32[]{:S(2)}, u32[]{:S(2)}) collective-permute-start(f32[24,8,256]{2,1,0:T(8,128)S(1)} %pad_maximum_fusion.1), channel_id=1, source_target_pairs={{0,8},{8,16},{16,24},{24,0},{1,9},{9,17},{17,25},{25,1},{2,10},{10... | collective-permute-start | bytes 589832 | tf_op jit(solution)/shard_map/ppermute | solution.py:203
  248.4 17.5 %collective-permute-start.10 = (f32[24,8,256]{2,1,0:T(8,128)S(1)}, f32[24,8,256]{2,1,0:T(8,128)S(1)}, u32[]{:S(2)}, u32[]{:S(2)}) collective-permute-start(f32[24,8,256]{2,1,0:T(8,128)S(1)} %pad_maximum_fusion.5), channel_id=1, source_target_pairs={{0,8},{8,16},{16,24},{24,0},{1,9},{9,17},{17,25},{25,1},{2,10},{10... | collective-permute-start | bytes 589832 | tf_op jit(solution)/shard_map/ppermute | solution.py:203
  250.9 18.3 %collective-permute-start.11 = (f32[24,8,256]{2,1,0:T(8,128)S(1)}, f32[24,8,256]{2,1,0:T(8,128)S(1)}, u32[]{:S(2)}, u32[]{:S(2)}) collective-permute-start(f32[24,8,256]{2,1,0:T(8,128)S(1)} %pad_maximum_fusion.6), channel_id=1, source_target_pairs={{0,24},{8,0},{16,8},{24,16},{1,25},{9,1},{17,9},{25,17},{2,26},{10... | collective-permute-start | bytes 589832 | tf_op jit(solution)/shard_map/ppermute | solution.py:203
  252.6 24.6 %collective-permute-start.6 = (f32[24,8,256]{2,1,0:T(8,128)S(1)}, f32[24,8,256]{2,1,0:T(8,128)S(1)}, u32[]{:S(2)}, u32[]{:S(2)}) collective-permute-start(f32[24,8,256]{2,1,0:T(8,128)S(1)} %pad_maximum_fusion.3), channel_id=1, source_target_pairs={{0,8},{8,16},{16,24},{24,0},{1,9},{9,17},{17,25},{25,1},{2,10},{10... | collective-permute-start | bytes 589832 | tf_op jit(solution)/shard_map/ppermute | solution.py:203
  256.6 21.1 %collective-permute-start.7 = (f32[24,8,256]{2,1,0:T(8,128)S(1)}, f32[24,8,256]{2,1,0:T(8,128)S(1)}, u32[]{:S(2)}, u32[]{:S(2)}) collective-permute-start(f32[24,8,256]{2,1,0:T(8,128)S(1)} %pad_maximum_fusion.4), channel_id=1, source_target_pairs={{0,24},{8,0},{16,8},{24,16},{1,25},{9,1},{17,9},{25,17},{2,26},{10... | collective-permute-start | bytes 589832 | tf_op jit(solution)/shard_map/ppermute | solution.py:203
  266.0 18.4 %collective-permute-start.3 = (f32[24,8,256]{2,1,0:T(8,128)S(1)}, f32[24,8,256]{2,1,0:T(8,128)S(1)}, u32[]{:S(2)}, u32[]{:S(2)}) collective-permute-start(f32[24,8,256]{2,1,0:T(8,128)S(1)} %pad_maximum_fusion.2), channel_id=1, source_target_pairs={{0,24},{8,0},{16,8},{24,16},{1,25},{9,1},{17,9},{25,17},{2,26},{10... | collective-permute-start | bytes 589832 | tf_op jit(solution)/shard_map/ppermute | solution.py:203
  314.5 53.5 %all-to-all-start.5 = ((f32[256,16,128]{2,1,0:T(8,128)}), f32[256,16,128]{2,1,0:T(8,128)}, u32[]{:S(2)}, u32[]{:S(2)}) async-start(f32[256,16,128]{2,1,0:T(8,128)} %copy.71), calls=%async_computation.5 | async-start | bytes 4194304 | tf_op jit(solution)/shard_map/all_to_all | solution.py:260
  368.0 53.5 %all-to-all-start.4 = ((f32[256,16,128]{2,1,0:T(8,128)}), f32[256,16,128]{2,1,0:T(8,128)}, u32[]{:S(2)}, u32[]{:S(2)}) async-start(f32[256,16,128]{2,1,0:T(8,128)} %copy.69), calls=%async_computation.4 | async-start | bytes 4194304 | tf_op jit(solution)/shard_map/all_to_all | solution.py:260
  421.5 53.5 %all-to-all-start.6 = ((f32[256,16,128]{2,1,0:T(8,128)}), f32[256,16,128]{2,1,0:T(8,128)}, u32[]{:S(2)}, u32[]{:S(2)}) async-start(f32[256,16,128]{2,1,0:T(8,128)} %copy.73), calls=%async_computation.6 | async-start | bytes 4194304 | tf_op jit(solution)/shard_map/all_to_all | solution.py:260
  475.0 52.8 %all-to-all-start.7 = ((f32[256,16,128]{2,1,0:T(8,128)}), f32[256,16,128]{2,1,0:T(8,128)S(1)}, u32[]{:S(2)}, u32[]{:S(2)}) async-start(f32[256,16,128]{2,1,0:T(8,128)} %copy.75), calls=%async_computation.7 | async-start | bytes 4194304 | tf_op jit(solution)/shard_map/all_to_all | solution.py:260
  (25 other events, 246.5 us)

commit v2 on v1

v2 whole, which is shorter than its diff:
```python
import functools

import jax
import jax.numpy as jnp
from jax import lax
from jax.experimental import pallas as pl
from jax.experimental.pallas import tpu as pltpu
from jax.sharding import PartitionSpec as P

PSIDE = 16
HALO = 4
ITERS = 5
SUB = 8
SPAN = PSIDE + 2 * HALO
HIGHEST = lax.Precision.HIGHEST
VMEM_LIMIT = 32 * 1024 * 1024
SMALL_LIMIT = 60 * 1024 * 1024


def split(x):
    high = x.astype(jnp.bfloat16)
    return high, (x - high.astype(jnp.float32)).astype(jnp.bfloat16)


def dot3(a, b, dims=((1,), (0,))):
    def one(x, y):
        return lax.dot_general(x, y, (dims, ((), ())), preferred_element_type=jnp.float32)

    return one(a[0], b[0]) + (one(a[0], b[1]) + one(a[1], b[0]))


def pack_kernel(ny, offset, width, source, out):
    levels = source.shape[1]
    lat = source.shape[2] // ny
    lon = source.shape[3] // out.shape[0]
    for x in range(out.shape[0]):
        begin = x * lon + offset
        parts = [source[0, level, :, begin : begin + width] for level in range(levels)]
        out[x, :, 0] = jnp.concatenate(parts, axis=1).reshape(ny, lat, levels * width)


def unpack_kernel(ny, *refs):
    *chunks, out = refs
    levels = out.shape[1]
    for x in range(chunks[0].shape[0]):
        for level in range(levels):
            begin = level * 2 * PSIDE
            parts = [chunks[-1][x, :, 0, :, begin + PSIDE : begin + 2 * PSIDE]]
            parts += [chunk[x, :, 0, :, begin : begin + 2 * PSIDE] for chunk in chunks[:-1]]
            parts += [chunks[-1][x, :, 0, :, begin : begin + PSIDE]]
            whole = jnp.concatenate(parts, axis=2)
            lon = whole.shape[2]
            out[0, level, :, x * lon : (x + 1) * lon] = whole.reshape(-1, lon)


def roots_of(grams, pulls, sweeps):
    members = grams[0].shape[0]
    eye = (
        lax.broadcasted_iota(jnp.int32, (members, members), 0)
        == lax.broadcasted_iota(jnp.int32, (members, members), 1)
    ).astype(jnp.float32)
    divisors, currents = [], []
    for g in grams:
        square = jnp.sum(jnp.sum(g * g, axis=0, keepdims=True), axis=1, keepdims=True)
        divisor = members - 1.0 + jnp.sqrt(square)
        divisors.append(divisor)
        currents.append((g + (members - 1.0) * eye) / divisor)
    roots = None
    for repeat in range(sweeps):
        cur = [split(c) for c in currents]
        if repeat == 0:
            factors = [1.5 * eye - 0.5 * c for c in currents]
            fac = [split(f) for f in factors]
            roots = factors
        else:
            old = [split(r) for r in roots]
            factors = [1.5 * eye - 0.5 * dot3(r, c) for r, c in zip(old, cur)]
            fac = [split(f) for f in factors]
            roots = [dot3(f, r) for f, r in zip(fac, old)]
        if repeat < sweeps - 1:
            currents = [dot3(c, f) for c, f in zip(cur, fac)]
    results = []
    for divisor, root, pull in zip(divisors, roots, pulls):
        half = jnp.sum(root * pull, axis=1, keepdims=True)
        mean = jnp.sum(root * half, axis=0, keepdims=True) / divisor
        results.append((split(jnp.sqrt((members - 1.0) / divisor) * root), mean))
    return results


def pair_kernel(inside, *refs):
    first, second, refs = refs[:3], refs[3:6], refs[6:]
    if inside:
        tables, out, gram, pulled = refs
    else:
        after, before, tables, out, gram, pulled = refs
    rows, lanes, members = first[1].shape
    levels = tables.shape[1]
    width = lanes // levels
    cells = SPAN * SUB
    cell_row = lax.broadcasted_iota(jnp.int32, (cells, SPAN), 0) // SUB
    expand = (cell_row == lax.broadcasted_iota(jnp.int32, (cells, SPAN), 1)).astype(jnp.float32)
    sub = lax.broadcasted_iota(jnp.int32, (cells, 2 * SPAN), 0) % SUB
    lane = lax.broadcasted_iota(jnp.int32, (cells, 2 * SPAN), 1)
    near = lax.broadcasted_iota(jnp.int32, (SPAN, SUB, members), 1) < HALO
    gram[...] = jnp.zeros_like(gram)
    pulled[...] = jnp.zeros_like(pulled)

    def step(level, carry):
        def block(group, offset):
            where = pl.ds(pl.multiple_of(level * width + offset, SUB), SUB)
            return jnp.concatenate([ref[:, where, :] for ref in group], axis=0)

        def outside(ref):
            return ref[:, pl.ds(pl.multiple_of(level * SUB, SUB), SUB), :]

        right = block(second, 0) if inside else outside(after)
        left = block(first, width - SUB) if inside else outside(before)
        both = [
            (
                block(first, PSIDE),
                block(first, PSIDE + SUB),
                jnp.where(near, right, block(first, PSIDE - SUB)),
            ),
            (block(second, 0), block(second, SUB), jnp.where(near, block(second, PSIDE), left)),
        ]
        for p, pieces in enumerate(both):
            table = jnp.dot(
                expand, tables[p, level], precision=HIGHEST, preferred_element_type=jnp.float32
            )
            spread, scaled, pull = [], [], 0.0
            for g, piece in enumerate(pieces):
                x = piece.reshape(cells, members)
                mean = jnp.mean(x, axis=1, keepdims=True)
                y = x - mean
                w = jnp.sum(jnp.where(lane == g * SUB + sub, table, 0.0), axis=1, keepdims=True)
                u = jnp.sum(
                    jnp.where(lane == SPAN + g * SUB + sub, table, 0.0), axis=1, keepdims=True
                )
                pull = pull + jnp.sum(y * (u - w * mean), axis=0, keepdims=True)
                spread.append(y)
                scaled.append(y * w)
            y = split(jnp.concatenate(spread, axis=0))
            z = split(jnp.concatenate(scaled, axis=0))
            gram[p] += dot3(z, y, ((0,), (0,)))
            pulled[p] += pull
        return carry

    lax.fori_loop(0, levels, step, 0)
    results = roots_of([gram[0], gram[1]], [pulled[0], pulled[1]], ITERS)
    for p, (group, offset) in enumerate(((first, PSIDE), (second, 0))):
        root, mean_weight = results[p]
        for level in range(levels):
            x = group[1][:, level * width + offset : level * width + offset + PSIDE, :]
            x = x.reshape(rows * PSIDE, members)
            centre = jnp.mean(x, axis=1, keepdims=True)
            d = x - centre
            moved = centre + jnp.sum(d * mean_weight, axis=1, keepdims=True)
            mixed = moved + dot3(split(d), root)
            begin = level * width + p * PSIDE
            out[:, begin : begin + PSIDE, :] = mixed.reshape(rows, PSIDE, members)


def estimate(flops, *arrays):
    moved = sum(a.size * a.dtype.itemsize for a in arrays)
    return pl.CostEstimate(flops=flops, bytes_accessed=moved, transcendentals=0)


def pack(background, nx, ny, offset, width):
    here, levels, lat_rows, lon_cells = background.shape
    lat = lat_rows // ny
    shape = jax.ShapeDtypeStruct((nx, ny, here, lat, levels * width), background.dtype)
    return pl.pallas_call(
        functools.partial(pack_kernel, ny, offset, width),
        out_shape=shape,
        grid=(here,),
        in_specs=[pl.BlockSpec((1, levels, lat_rows, lon_cells), lambda h: (h, 0, 0, 0))],
        out_specs=pl.BlockSpec((nx, ny, 1, lat, levels * width), lambda h: (0, 0, h, 0, 0)),
        cost_estimate=estimate(0, background, shape),
        compiler_params=pltpu.CompilerParams(vmem_limit_bytes=SMALL_LIMIT),
    )(background)


def unpack(chunks, shape):
    nx, ny, here, lat, lanes = chunks[0].shape
    return pl.pallas_call(
        functools.partial(unpack_kernel, ny),
        out_shape=jax.ShapeDtypeStruct(shape, chunks[0].dtype),
        grid=(here,),
        in_specs=[pl.BlockSpec((nx, ny, 1, lat, lanes), lambda h: (0, 0, h, 0, 0))] * len(chunks),
        out_specs=pl.BlockSpec((1, *shape[1:]), lambda h: (h, 0, 0, 0)),
        cost_estimate=estimate(0, *chunks, *chunks),
        compiler_params=pltpu.CompilerParams(vmem_limit_bytes=SMALL_LIMIT),
    )(*chunks)


def analyse(inside, inputs, levels):
    core = inputs[1]
    members = core.shape[2]
    shape = jax.ShapeDtypeStruct(core.shape, core.dtype)
    vmem = pl.BlockSpec(memory_space=pltpu.VMEM)
    flops = 6 * 2 * members**2 * (levels * SPAN * SPAN + levels * PSIDE * PSIDE + 12 * members)
    return pl.pallas_call(
        functools.partial(pair_kernel, inside),
        out_shape=shape,
        in_specs=[vmem] * len(inputs),
        out_specs=vmem,
        scratch_shapes=[
            pltpu.VMEM((2, members, members), jnp.float32),
            pltpu.VMEM((2, 1, members), jnp.float32),
        ],
        cost_estimate=estimate(5 * flops, *inputs, shape),
        compiler_params=pltpu.CompilerParams(vmem_limit_bytes=VMEM_LIMIT),
    )(*inputs)


def tables_of(obs_cells, obs_counts, obs_widths, obs_values, obs_variances, levels):
    level_of = obs_cells // (SPAN * SPAN)
    row = obs_cells // SPAN % SPAN
    col = obs_cells % SPAN
    row_out = jnp.maximum(jnp.maximum(HALO - row, row - (HALO + PSIDE - 1)), 0)
    col_out = jnp.maximum(jnp.maximum(HALO - col, col - (HALO + PSIDE - 1)), 0)
    distance = jnp.maximum(row_out, col_out)
    slots = lax.broadcasted_iota(jnp.int32, obs_cells.shape, 1)
    usable = (slots < obs_counts[:, None]) & (distance <= obs_widths[:, None])
    relative = distance.astype(jnp.float32) / (obs_widths[:, None] + 1).astype(jnp.float32)
    weights = jnp.where(usable, jnp.exp(-relative * relative) / obs_variances, 0.0)
    place = jnp.where(
        col < HALO,
        PSIDE + HALO + col,
        col - HALO,
    )
    line = level_of * SPAN + row
    hot_line = (line[:, :, None] == jnp.arange(levels * SPAN)).astype(jnp.float32)
    hot_place = place[:, :, None] == jnp.arange(SPAN)
    sums = jnp.concatenate(
        [
            jnp.where(hot_place, weights[:, :, None], 0.0),
            jnp.where(hot_place, (weights * obs_values)[:, :, None], 0.0),
        ],
        axis=2,
    )
    table = jnp.einsum("psl,psg->plg", hot_line, sums, precision=HIGHEST)
    return table.reshape(table.shape[0], levels, SPAN, 2 * SPAN)


def shift(x, axis, step, wrap):
    n = lax.axis_size(axis)
    pairs = [(i, (i + step) % n) for i in range(n) if wrap or 0 <= i + step < n]
    return lax.ppermute(x, axis, pairs)


def shards(background, obs_cells, obs_counts, obs_widths, obs_values, obs_variances):
    here, levels, lat_rows, lon_cells = background.shape
    nx = lax.axis_size("gx")
    ny = lax.axis_size("gy")
    lat = lat_rows // ny
    lon = lon_cells // nx
    members = nx * ny * here
    width = 2 * PSIDE
    number = lon // width
    tables = tables_of(
        obs_cells[0], obs_counts[0], obs_widths[0], obs_values[0], obs_variances[0], levels
    )

    def exchange(x):
        return lax.all_to_all(x, ("gx", "gy"), split_axis=0, concat_axis=0, tiled=True)

    def section(group, begin):
        def pick(x):
            x = x.reshape(x.shape[0], levels, width, members)[:, :, begin : begin + SUB]
            return x.reshape(x.shape[0], levels * SUB, members)

        return jnp.concatenate([pick(x) for x in group], axis=0)

    packed = [
        pack(background, nx, ny, q * width, width).reshape(members, lat, levels * width)
        for q in range(number)
    ]
    groups, mixed = [], []
    for q in range(number):
        send = packed[q]
        if q >= 3:
            send, mixed[q - 3] = lax.optimization_barrier((send, mixed[q - 3]))
        gathered = exchange(send)
        core = jnp.transpose(gathered, (1, 2, 0))
        up = shift(core[lat - HALO :], "gy", 1, False)
        down = shift(core[:HALO], "gy", -1, False)
        groups.append((up, core, down))
        if q == 0:
            after = shift(section(groups[0], 0), "gx", -1, True)
        if q in range(1, number - 1):
            table = tables[2 * q - 1 : 2 * q + 1]
            mixed.append(analyse(True, (*groups[q - 1], *groups[q], table), levels))
    q = number - 1
    mixed[0], gathered, mixed[-1] = lax.optimization_barrier((mixed[0], gathered, mixed[-1]))
    before = shift(section(groups[-1], width - SUB), "gx", 1, True)
    table = tables[2 * q - 1 : 2 * q + 1]
    mixed.append(analyse(True, (*groups[q - 1], *groups[q], table), levels))
    table = jnp.stack([tables[-1], tables[0]])
    mixed.append(analyse(False, (*groups[-1], *groups[0], after, before, table), levels))
    chunks = []
    for c in range(number):
        back = jnp.transpose(mixed[c], (2, 0, 1))
        if 0 < c < number - 1:
            back, mixed[c + 1] = lax.optimization_barrier((back, mixed[c + 1]))
        chunks.append(exchange(back).reshape(nx, ny, here, lat, levels * width))
    return unpack(chunks, background.shape)


def solution(mesh):
    return jax.shard_map(
        shards,
        mesh=mesh,
        in_specs=(
            P(("gx", "gy"), None, None, None),
            P("gy", "gx", None),
            P("gy", "gx"),
            P("gy", "gx"),
            P("gy", "gx", None),
            P("gy", "gx", None),
        ),
        out_specs=P(("gx", "gy"), None, None, None),
        check_vma=False,
    )
```

time: 543 us -> 561 us (1.033)
  waiting for transfers between devices: 318 us -> 232 us
  starting transfers between devices: 56.7 us -> 118 us
  blocking collectives: 0 us -> 53.4 us
  local copies, waits for them, and re-layouts: 102 us -> 52.9 us
  Pallas kernels: 58.6 us -> 95.1 us
    all_to_all x8 -> x7, waiting for transfers between devices: 311 us -> 175 us  [exchange(): lax.all_to_all(x, ('gx', 'gy'), split_axis=0, concat_axis=0, tiled=True)]
    all_to_all x8 -> x7, starting transfers between devices: 30.5 us -> 97.5 us  [exchange(): lax.all_to_all(x, ('gx', 'gy'), split_axis=0, concat_axis=0, tiled=True)]
    all_to_all x0 -> x1, blocking collectives: none -> 53.4 us  [exchange(): lax.all_to_all(x, ('gx', 'gy'), split_axis=0, concat_axis=0, tiled=True)]
    ppermute x16 -> x10, waiting for transfers between devices: 7.38 us -> 56.5 us  [shift(): return lax.ppermute(x, axis, pairs)]
    pallas_call x9, Pallas kernels: 58.6 us -> 95.1 us  [the longest x4 50.5 us: analyse(): pl.pallas_call(functools.partial(pair_kernel, inside), out_shape=shape, i...]
    transpose x12 -> x2, local copies, waits for them, and re-layouts: 37.4 us -> 4.99 us  [shards(): back = jnp.transpose(mixed[c], (2, 0, 1))]
    another operation x9 -> x0, local copies, waits for them, and re-layouts: 26.5 us -> none  [the longest x5 16.8 us: shards(): return jnp.stack(results, axis=1)]
    slice x13 -> x7, local copies, waits for them, and re-layouts: 14.1 us -> 1.2 us  [the longest x3 0.93 us: shards(): table = jnp.stack([tables[-1], tables[0]])]
  transfers between devices with their start and end apart: 24 -> 17, of which waited for: 12 -> 10; matrix products, arithmetic and copies ran while one was open for 13% -> 7% of each run, Pallas kernels for 6% -> 13%
where the time goes in v2:
time: 561 us; the launch traced here: 559 us
  waiting for transfers between devices  232 us (41%)
  starting transfers between devices  118 us (21%)
  Pallas kernels  95.1 us (17%)
  blocking collectives  53.4 us (10%)
  local copies, waits for them, and re-layouts  52.9 us (9%)
    all_to_all x7, waiting for transfers between devices, exchange(): lax.all_to_all(x, ('gx', 'gy'), split_axis=0, concat_axis=0, tiled=True)  175 us
    all_to_all x7, starting transfers between devices, exchange(): lax.all_to_all(x, ('gx', 'gy'), split_axis=0, concat_axis=0, tiled=True)  97.5 us
    ppermute x10, waiting for transfers between devices, shift(): return lax.ppermute(x, axis, pairs)  56.5 us
    all_to_all x1, blocking collectives, exchange(): lax.all_to_all(x, ('gx', 'gy'), split_axis=0, concat_axis=0, tiled=True)  53.4 us
    pallas_call x4, Pallas kernels, analyse(): pl.pallas_call(functools.partial(pair_kernel, inside), out_shape=shape, i...  50.5 us
    pallas_call x4, Pallas kernels, pack(): pl.pallas_call(functools.partial(pack_kernel, ny, offset, width), out_sha...  31.6 us
    ppermute x10, starting transfers between devices, shift(): return lax.ppermute(x, axis, pairs)  20.1 us
    unnamed x46, local copies, waits for them, and re-layouts  19 us
  transfers between devices with their start and end apart: 17, of which 10 were waited for; matrix products, arithmetic and copies ran while one was open for 7% of the time, Pallas kernels for 13%

profile of v2, /device:TPU:0, one launch (start us, length us, event | category | flops | bytes accessed | tf_op | source)
XLA Modules:
  0.0 558.9 jit_solution(2873904242119018985)
XLA Ops:
  0.0 7.9 %shard_map.65 = f32[4,8,8,16,128]{4,3,2,1,0:T(8,128)} custom-call(f32[8,4,128,512]{3,2,1,0:T(8,128)} %source.7), custom_call_target="tpu_custom_call" | custom-call | bytes 10485760 | tf_op jit(solution)/shard_map/pallas_call | solution.py:172
  7.9 7.3 %all-to-all-start = ((f32[256,16,128]{2,1,0:T(8,128)}), f32[256,16,128]{2,1,0:T(8,128)S(1)}, u32[]{:S(2)}, u32[]{:S(2)}) async-start(f32[256,16,128]{2,1,0:T(8,128)} %bitcast.122), calls=%async_computation | async-start | bytes 4194304 | tf_op jit(solution)/shard_map/all_to_all | solution.py:266
  15.2 7.9 %shard_map.66 = f32[4,8,8,16,128]{4,3,2,1,0:T(8,128)} custom-call(f32[8,4,128,512]{3,2,1,0:T(8,128)} %source.7), custom_call_target="tpu_custom_call" | custom-call | bytes 10485760 | tf_op jit(solution)/shard_map/pallas_call | solution.py:172
  23.1 42.1 %all-to-all-done = f32[256,16,128]{2,1,0:T(8,128)S(1)} async-done(((f32[256,16,128]{2,1,0:T(8,128)}), f32[256,16,128]{2,1,0:T(8,128)S(1)}, u32[]{:S(2)}, u32[]{:S(2)}) %all-to-all-start) | async-done | bytes 2097184 | tf_op jit(solution)/shard_map/all_to_all | solution.py:266
  69.3 7.9 %shard_map.68 = f32[4,8,8,16,128]{4,3,2,1,0:T(8,128)} custom-call(f32[8,4,128,512]{3,2,1,0:T(8,128)} %source.7), custom_call_target="tpu_custom_call" | custom-call | bytes 10485760 | tf_op jit(solution)/shard_map/pallas_call | solution.py:172
  77.3 42.0 %all-to-all-done.1 = f32[256,16,128]{2,1,0:T(8,128)S(1)} async-done(((f32[256,16,128]{2,1,0:T(8,128)}), f32[256,16,128]{2,1,0:T(8,128)S(1)}, u32[]{:S(2)}, u32[]{:S(2)}) %all-to-all-start.1) | async-done | bytes 2097184 | tf_op jit(solution)/shard_map/all_to_all | solution.py:266
  120.7 3.5 all-to-all-start.3
  135.8 5.0 collective-permute-start.2
  143.5 8.0 %shard_map.64 = f32[4,8,8,16,128]{4,3,2,1,0:T(8,128)} custom-call(f32[8,4,128,512]{3,2,1,0:T(8,128)} %source.7), custom_call_target="tpu_custom_call" | custom-call | bytes 10485760 | tf_op jit(solution)/shard_map/pallas_call | solution.py:172
  156.9 12.5 %shard_map.67 = f32[16,128,256]{2,1,0:T(8,128)S(1)} custom-call(f32[4,128,256]{2,1,0:T(8,128)S(1)} %collective-permute-done.refs_0_.refs_3_, f32[16,128,256]{2,1,0:T(8,128)S(1)} %bitcast.95, f32[4,128,256]{2,1,0:T(8,128)S(1)} %collective-permute-done.1.refs_2_.refs_5_, f32[4,128,256]{2,1,0:T(8,128)} %collective-permute-done.2.refs_3_.refs_0_, ...), custom_call_target="tpu_custom_call" | custom-call | flops 25165824000 | bytes 8425472 | tf_op jit(solution)/shard_map/pallas_call | solution.py:202
  174.2 28.0 %all-to-all-start.2 = ((f32[256,16,128]{2,1,0:T(8,128)}), f32[256,16,128]{2,1,0:T(8,128)}, u32[]{:S(2)}, u32[]{:S(2)}) async-start(f32[256,16,128]{2,1,0:T(8,128)} %bitcast.120), calls=%async_computation.2 | async-start | bytes 4194304 | tf_op jit(solution)/shard_map/all_to_all | solution.py:266
  218.0 12.8 %shard_map.69 = f32[16,128,256]{2,1,0:T(8,128)S(1)} custom-call(f32[4,128,256]{2,1,0:T(8,128)} %collective-permute-done.2.refs_3_.refs_0_, f32[16,128,256]{2,1,0:T(8,128)S(1)} %bitcast.104, f32[4,128,256]{2,1,0:T(8,128)} %collective-permute-done.3.refs_5_.refs_2_, f32[4,128,256]{2,1,0:T(8,128)} %collective-permute-done.4.refs_3_.refs_0_, ...), custom_call_target="tpu_custom_call" | custom-call | flops 25165824000 | bytes 8425472 | tf_op jit(solution)/shard_map/pallas_call | solution.py:202
  232.3 19.9 %all-to-all-done.2 = f32[256,16,128]{2,1,0:T(8,128)} async-done(((f32[256,16,128]{2,1,0:T(8,128)}), f32[256,16,128]{2,1,0:T(8,128)}, u32[]{:S(2)}, u32[]{:S(2)}) %all-to-all-start.2) | async-done | bytes 2097184 | tf_op jit(solution)/shard_map/all_to_all | solution.py:266
  255.3 24.6 %all-to-all-start.4 = ((f32[256,16,128]{2,1,0:T(8,128)}), f32[256,16,128]{2,1,0:T(8,128)}, u32[]{:S(2)}, u32[]{:S(2)}) async-start(f32[256,16,128]{2,1,0:T(8,128)} %copy.38), calls=%async_computation.4 | async-start | bytes 4194304 | tf_op jit(solution)/shard_map/all_to_all | solution.py:266
  293.1 12.5 %shard_map.70 = f32[16,128,256]{2,1,0:T(8,128)S(1)} custom-call(f32[4,128,256]{2,1,0:T(8,128)} %collective-permute-done.4.refs_3_.refs_0_, f32[16,128,256]{2,1,0:T(8,128)S(1)} %bitcast.107, f32[4,128,256]{2,1,0:T(8,128)} %collective-permute-done.5.refs_5_.refs_2_, f32[4,128,256]{2,1,0:T(8,128)S(1)} %collective-permute-done.6.refs_3_.refs_0_, ...), custom_call_target="tpu_custom_call" | custom-call | flops 25165824000 | bytes 8425472 | tf_op jit(solution)/shard_map/pallas_call | solution.py:202
  310.1 19.8 %all-to-all-done.4 = f32[256,16,128]{2,1,0:T(8,128)} async-done(((f32[256,16,128]{2,1,0:T(8,128)}), f32[256,16,128]{2,1,0:T(8,128)}, u32[]{:S(2)}, u32[]{:S(2)}) %all-to-all-start.4) | async-done | bytes 2097184 | tf_op jit(solution)/shard_map/all_to_all | solution.py:266
  329.9 25.9 %all-to-all-start.5 = ((f32[256,16,128]{2,1,0:T(8,128)}), f32[256,16,128]{2,1,0:T(8,128)}, u32[]{:S(2)}, u32[]{:S(2)}) async-start(f32[256,16,128]{2,1,0:T(8,128)} %copy.41), calls=%async_computation.5 | async-start | bytes 4194304 | tf_op jit(solution)/shard_map/all_to_all | solution.py:266
  365.3 31.5 %collective-permute-done.8.refs_6_ = f32[24,32,256]{2,1,0:T(8,128)} collective-permute-done((f32[24,32,256]{2,1,0:T(8,128)}, f32[24,32,256]{2,1,0:T(8,128)}, u32[]{:S(2)}, u32[]{:S(2)}) %collective-permute-start.8) | collective-permute-done | bytes 786464 | tf_op jit(solution)/shard_map/ppermute | solution.py:249
  396.8 19.6 %collective-permute-done.9.refs_7_ = f32[24,32,256]{2,1,0:T(8,128)} collective-permute-done((f32[24,32,256]{2,1,0:T(8,128)}, f32[24,32,256]{2,1,0:T(8,128)}, u32[]{:S(2)}, u32[]{:S(2)}) %collective-permute-start.9) | collective-permute-done | bytes 786464 | tf_op jit(solution)/shard_map/ppermute | solution.py:249
  420.1 12.7 %shard_map.71 = f32[16,128,256]{2,1,0:T(8,128)S(1)} custom-call(f32[4,128,256]{2,1,0:T(8,128)S(1)} %copy-done.12, f32[16,128,256]{2,1,0:T(8,128)S(1)} %bitcast.101, f32[4,128,256]{2,1,0:T(8,128)S(1)} %copy-done.14, f32[4,128,256]{2,1,0:T(8,128)S(1)} %collective-permute-done.refs_0_.refs_3_, f32[16,128,256]{2,1,0:T(8,128)S(1)} %bitcast.97, ...), custom_call_target="tpu_custom_call" | custom-call | flops 25165824000 | bytes 9998336 | tf_op jit(solution)/shard_map/pallas_call | solution.py:202
  437.2 5.4 all-to-all-start.6
  444.6 48.0 %all-to-all-done.6 = f32[256,16,128]{2,1,0:T(8,128)} async-done(((f32[256,16,128]{2,1,0:T(8,128)}), f32[256,16,128]{2,1,0:T(8,128)}, u32[]{:S(2)}, u32[]{:S(2)}) %all-to-all-start.6) | async-done | bytes 2097184 | tf_op jit(solution)/shard_map/all_to_all | solution.py:266
  492.6 53.4 %all_to_all.40 = f32[256,16,128]{2,1,0:T(8,128)} all-to-all(f32[256,16,128]{2,1,0:T(8,128)} %copy.45), channel_id=1, replica_groups=mesh['gx'=4,'gy'=8] {'gx','gy'}, dimensions={0} | all-to-all | bytes 4194304 | tf_op jit(solution)/shard_map/all_to_all | solution.py:266
  546.0 12.9 %shard_map.72 = f32[8,4,128,512]{3,2,1,0:T(8,128)} custom-call(f32[4,8,8,16,128]{4,3,2,1,0:T(8,128)} %bitcast.19.refs_0_, f32[4,8,8,16,128]{4,3,2,1,0:T(8,128)} %bitcast.23.refs_1_, f32[4,8,8,16,128]{4,3,2,1,0:T(8,128)} %bitcast.39.refs_2_, f32[4,8,8,16,128]{4,3,2,1,0:T(8,128)} %bitcast.123), custom_call_target="tpu_custom_call" | custom-call | bytes 16777216 | tf_op jit(solution)/shard_map/pallas_call | solution.py:185
  (99 shorter events, 87.3 us)
Async XLA Ops:
  7.9 57.4 %all-to-all-start = ((f32[256,16,128]{2,1,0:T(8,128)}), f32[256,16,128]{2,1,0:T(8,128)S(1)}, u32[]{:S(2)}, u32[]{:S(2)}) async-start(f32[256,16,128]{2,1,0:T(8,128)} %bitcast.122), calls=%async_computation | async-start | bytes 4194304 | tf_op jit(solution)/shard_map/all_to_all | solution.py:266
  66.5 52.8 %all-to-all-start.1 = ((f32[256,16,128]{2,1,0:T(8,128)}), f32[256,16,128]{2,1,0:T(8,128)S(1)}, u32[]{:S(2)}, u32[]{:S(2)}) async-start(f32[256,16,128]{2,1,0:T(8,128)} %bitcast.121), calls=%async_computation.1 | async-start | bytes 4194304 | tf_op jit(solution)/shard_map/all_to_all | solution.py:266
  69.3 7.9 %copy-start.18 = (s32[1,8,1024]{2,1,0:T(8,128)S(1)}, s32[1,8,1024]{2,1,0:T(8,128)}, u32[]{:S(2)}) copy-start(s32[1,8,1024]{2,1,0:T(8,128)} %param.7) | copy-start | bytes 98308
  119.3 4.9 copy-start.20
  119.3 4.9 copy-start.22
  120.7 53.5 %all-to-all-start.3 = ((f32[256,16,128]{2,1,0:T(8,128)}), f32[256,16,128]{2,1,0:T(8,128)}, u32[]{:S(2)}, u32[]{:S(2)}) async-start(f32[256,16,128]{2,1,0:T(8,128)} %bitcast.119), calls=%async_computation.3 | async-start | bytes 4194304 | tf_op jit(solution)/shard_map/all_to_all | solution.py:266
  127.4 27.9 %collective-permute-start = (f32[4,128,256]{2,1,0:T(8,128)}, f32[4,128,256]{2,1,0:T(8,128)S(1)}, u32[]{:S(2)}, u32[]{:S(2)}) collective-permute-start(f32[4,128,256]{2,1,0:T(8,128)} %get-tuple-element.30), channel_id=1, source_target_pairs={{0,1},{1,2},{2,3},{3,4},{4,5},{5,6},{6,7},{8,9},{9,10},{10,11},{11... | collective-permute-start | bytes 1572872 | tf_op jit(solution)/shard_map/ppermute | solution.py:249
  129.3 26.0 %collective-permute-start.1 = (f32[4,128,256]{2,1,0:T(8,128)}, f32[4,128,256]{2,1,0:T(8,128)S(1)}, u32[]{:S(2)}, u32[]{:S(2)}) collective-permute-start(f32[4,128,256]{2,1,0:T(8,128)} %get-tuple-element.29), channel_id=1, source_target_pairs={{1,0},{2,1},{3,2},{4,3},{5,4},{6,5},{7,6},{9,8},{10,9},{11,10},{12... | collective-permute-start | bytes 1572872 | tf_op jit(solution)/shard_map/ppermute | solution.py:249
  135.8 19.5 %collective-permute-start.2 = (f32[4,128,256]{2,1,0:T(8,128)}, f32[4,128,256]{2,1,0:T(8,128)}, u32[]{:S(2)}, u32[]{:S(2)}) collective-permute-start(f32[4,128,256]{2,1,0:T(8,128)} %get-tuple-element.28), channel_id=1, source_target_pairs={{0,1},{1,2},{2,3},{3,4},{4,5},{5,6},{6,7},{8,9},{9,10},{10,11},{11... | collective-permute-start | bytes 1572872 | tf_op jit(solution)/shard_map/ppermute | solution.py:249
  140.8 14.5 %collective-permute-start.3 = (f32[4,128,256]{2,1,0:T(8,128)}, f32[4,128,256]{2,1,0:T(8,128)}, u32[]{:S(2)}, u32[]{:S(2)}) collective-permute-start(f32[4,128,256]{2,1,0:T(8,128)} %get-tuple-element.27), channel_id=1, source_target_pairs={{1,0},{2,1},{3,2},{4,3},{5,4},{6,5},{7,6},{9,8},{10,9},{11,10},{12... | collective-permute-start | bytes 1572872 | tf_op jit(solution)/shard_map/ppermute | solution.py:249
  174.2 78.1 %all-to-all-start.2 = ((f32[256,16,128]{2,1,0:T(8,128)}), f32[256,16,128]{2,1,0:T(8,128)}, u32[]{:S(2)}, u32[]{:S(2)}) async-start(f32[256,16,128]{2,1,0:T(8,128)} %bitcast.120), calls=%async_computation.2 | async-start | bytes 4194304 | tf_op jit(solution)/shard_map/all_to_all | solution.py:266
  207.5 4.4 collective-permute-start.4
  210.4 4.5 collective-permute-start.5
  255.3 74.6 %all-to-all-start.4 = ((f32[256,16,128]{2,1,0:T(8,128)}), f32[256,16,128]{2,1,0:T(8,128)}, u32[]{:S(2)}, u32[]{:S(2)}) async-start(f32[256,16,128]{2,1,0:T(8,128)} %copy.38), calls=%async_computation.4 | async-start | bytes 4194304 | tf_op jit(solution)/shard_map/all_to_all | solution.py:266
  282.9 8.5 %copy-start = (f32[256,16,128]{0,2,1:T(8,128)S(1)}, f32[256,16,128]{0,2,1:T(8,128)}, u32[]{:S(2)}) copy-start(f32[256,16,128]{0,2,1:T(8,128)} %copy.39) | copy-start | bytes 6291460
  284.3 4.5 collective-permute-start.6
  286.4 4.9 collective-permute-start.7
  288.9 16.8 %copy-start.11 = (f32[4,128,256]{2,1,0:T(8,128)}, f32[4,128,256]{2,1,0:T(8,128)S(1)}, u32[]{:S(2)}) copy-start(f32[4,128,256]{2,1,0:T(8,128)S(1)} %collective-permute-done.6.refs_3_.refs_0_) | copy-start | bytes 1572868
  291.4 14.3 %copy-start.13 = (f32[4,128,256]{2,1,0:T(8,128)}, f32[4,128,256]{2,1,0:T(8,128)S(1)}, u32[]{:S(2)}) copy-start(f32[4,128,256]{2,1,0:T(8,128)S(1)} %collective-permute-done.7.refs_5_.refs_2_) | copy-start | bytes 1572868
  329.9 107.4 %all-to-all-start.5 = ((f32[256,16,128]{2,1,0:T(8,128)}), f32[256,16,128]{2,1,0:T(8,128)}, u32[]{:S(2)}, u32[]{:S(2)}) async-start(f32[256,16,128]{2,1,0:T(8,128)} %copy.41), calls=%async_computation.5 | async-start | bytes 4194304 | tf_op jit(solution)/shard_map/all_to_all | solution.py:266
  357.8 39.0 %collective-permute-start.8 = (f32[24,32,256]{2,1,0:T(8,128)}, f32[24,32,256]{2,1,0:T(8,128)}, u32[]{:S(2)}, u32[]{:S(2)}) collective-permute-start(f32[24,32,256]{2,1,0:T(8,128)} %pad_maximum_fusion), channel_id=1, source_target_pairs={{0,24},{8,0},{16,8},{24,16},{1,25},{9,1},{17,9},{25,17},{2,26},{10... | collective-permute-start | bytes 2359304 | tf_op jit(solution)/shard_map/ppermute | solution.py:249
  364.4 52.0 %collective-permute-start.9 = (f32[24,32,256]{2,1,0:T(8,128)}, f32[24,32,256]{2,1,0:T(8,128)}, u32[]{:S(2)}, u32[]{:S(2)}) collective-permute-start(f32[24,32,256]{2,1,0:T(8,128)} %pad_maximum_fusion.1), channel_id=1, source_target_pairs={{0,8},{8,16},{16,24},{24,0},{1,9},{9,17},{17,25},{25,1},{2,10},{10... | collective-permute-start | bytes 2359304 | tf_op jit(solution)/shard_map/ppermute | solution.py:249
  437.2 5.4 copy-start.10
  437.2 55.4 %all-to-all-start.6 = ((f32[256,16,128]{2,1,0:T(8,128)}), f32[256,16,128]{2,1,0:T(8,128)}, u32[]{:S(2)}, u32[]{:S(2)}) async-start(f32[256,16,128]{2,1,0:T(8,128)} %copy.44), calls=%async_computation.6 | async-start | bytes 4194304 | tf_op jit(solution)/shard_map/all_to_all | solution.py:266
  (16 other events, 28.8 us)

commit v3 on v2

--- a/solution.py
+++ b/solution.py
@@ -29,28 +29,35 @@
     return one(a[0], b[0]) + (one(a[0], b[1]) + one(a[1], b[0]))
 
 
-def pack_kernel(ny, offset, width, source, out):
+def pack_kernel(ny, turn, width, source, out):
     levels = source.shape[1]
     lat = source.shape[2] // ny
     lon = source.shape[3] // out.shape[0]
+    shape = (source.shape[2], lon)
+    group = lax.broadcasted_iota(jnp.int32, shape, 1) // width
     for x in range(out.shape[0]):
-        begin = x * lon + offset
-        parts = [source[0, level, :, begin : begin + width] for level in range(levels)]
-        out[x, :, 0] = jnp.concatenate(parts, axis=1).reshape(ny, lat, levels * width)
-
-
-def unpack_kernel(ny, *refs):
+        whole = source[0, 0, :, x * lon : (x + 1) * lon]
+        for level in range(1, levels):
+            part = source[0, level, :, x * lon : (x + 1) * lon]
+            part = pltpu.roll(part, level * width, 1)
+            whole = jnp.where(group == (turn + level) % levels, part, whole)
+        out[x, :, 0] = whole.reshape(ny, lat, lon)
+
+
+def unpack_kernel(*refs):
     *chunks, out = refs
     levels = out.shape[1]
+    ny, lat, lon = chunks[0].shape[1], chunks[0].shape[3], chunks[0].shape[4]
+    width = lon // levels
+    group = lax.broadcasted_iota(jnp.int32, (ny * lat, lon), 1) // width
     for x in range(chunks[0].shape[0]):
+        parts = [chunk[x, :, 0].reshape(ny * lat, lon) for chunk in chunks]
         for level in range(levels):
-            begin = level * 2 * PSIDE
-            parts = [chunks[-1][x, :, 0, :, begin + PSIDE : begin + 2 * PSIDE]]
-            parts += [chunk[x, :, 0, :, begin : begin + 2 * PSIDE] for chunk in chunks[:-1]]
-            parts += [chunks[-1][x, :, 0, :, begin : begin + PSIDE]]
-            whole = jnp.concatenate(parts, axis=2)
-            lon = whole.shape[2]
-            out[0, level, :, x * lon : (x + 1) * lon] = whole.reshape(-1, lon)
+            whole = parts[0]
+            for turn in range(1, len(parts)):
+                whole = jnp.where(group == (turn + level) % levels, parts[turn], whole)
+            back = (PSIDE - level * width) % lon
+            out[0, level, :, x * lon : (x + 1) * lon] = pltpu.roll(whole, back, 1)
 
 
 def roots_of(grams, pulls, sweeps):
@@ -87,13 +94,13 @@
     return results
 
 
-def pair_kernel(inside, *refs):
-    first, second, refs = refs[:3], refs[3:6], refs[6:]
+def pair_kernel(turn, inside, *refs):
+    first, second, refs = (refs[:3], turn), (refs[3:6], turn + 1), refs[6:]
     if inside:
-        tables, out, gram, pulled = refs
+        tables, _, out, gram, pulled = refs
     else:
-        after, before, tables, out, gram, pulled = refs
-    rows, lanes, members = first[1].shape
+        after, before, tables, _, out, gram, pulled = refs
+    rows, lanes, members = first[0][1].shape
     levels = tables.shape[1]
     width = lanes // levels
     cells = SPAN * SUB
@@ -107,8 +114,9 @@
 
     def step(level, carry):
         def block(group, offset):
-            where = pl.ds(pl.multiple_of(level * width + offset, SUB), SUB)
-            return jnp.concatenate([ref[:, where, :] for ref in group], axis=0)
+            begin = (level + group[1]) % levels * width + offset
+            where = pl.ds(pl.multiple_of(begin, SUB), SUB)
+            return jnp.concatenate([ref[:, where, :] for ref in group[0]], axis=0)
 
         def outside(ref):
             return ref[:, pl.ds(pl.multiple_of(level * SUB, SUB), SUB), :]
@@ -150,13 +158,14 @@
     for p, (group, offset) in enumerate(((first, PSIDE), (second, 0))):
         root, mean_weight = results[p]
         for level in range(levels):
-            x = group[1][:, level * width + offset : level * width + offset + PSIDE, :]
+            begin = (level + group[1]) % levels * width + offset
+            x = group[0][1][:, begin : begin + PSIDE, :]
             x = x.reshape(rows * PSIDE, members)
             centre = jnp.mean(x, axis=1, keepdims=True)
             d = x - centre
             moved = centre + jnp.sum(d * mean_weight, axis=1, keepdims=True)
             mixed = moved + dot3(split(d), root)
-            begin = level * width + p * PSIDE
+            begin = (level + turn) % levels * width + p * PSIDE
             out[:, begin : begin + PSIDE, :] = mixed.reshape(rows, PSIDE, members)
 
 
@@ -165,12 +174,12 @@
     return pl.CostEstimate(flops=flops, bytes_accessed=moved, transcendentals=0)
 
 
-def pack(background, nx, ny, offset, width):
+def pack(background, nx, ny, turn, width):
     here, levels, lat_rows, lon_cells = background.shape
     lat = lat_rows // ny
     shape = jax.ShapeDtypeStruct((nx, ny, here, lat, levels * width), background.dtype)
     return pl.pallas_call(
-        functools.partial(pack_kernel, ny, offset, width),
+        functools.partial(pack_kernel, ny, turn, width),
         out_shape=shape,
         grid=(here,),
         in_specs=[pl.BlockSpec((1, levels, lat_rows, lon_cells), lambda h: (h, 0, 0, 0))],
@@ -183,7 +192,7 @@
 def unpack(chunks, shape):
     nx, ny, here, lat, lanes = chunks[0].shape
     return pl.pallas_call(
-        functools.partial(unpack_kernel, ny),
+        unpack_kernel,
         out_shape=jax.ShapeDtypeStruct(shape, chunks[0].dtype),
         grid=(here,),
         in_specs=[pl.BlockSpec((nx, ny, 1, lat, lanes), lambda h: (0, 0, h, 0, 0))] * len(chunks),
@@ -193,22 +202,22 @@
     )(*chunks)
 
 
-def analyse(inside, inputs, levels):
+def analyse(turn, inside, inputs, levels):
     core = inputs[1]
     members = core.shape[2]
     shape = jax.ShapeDtypeStruct(core.shape, core.dtype)
     vmem = pl.BlockSpec(memory_space=pltpu.VMEM)
     flops = 6 * 2 * members**2 * (levels * SPAN * SPAN + levels * PSIDE * PSIDE + 12 * members)
     return pl.pallas_call(
-        functools.partial(pair_kernel, inside),
+        functools.partial(pair_kernel, turn, inside),
         out_shape=shape,
-        in_specs=[vmem] * len(inputs),
+        in_specs=[vmem] * (len(inputs) - 1) + [pl.BlockSpec(memory_space=pltpu.HBM)],
         out_specs=vmem,
         scratch_shapes=[
             pltpu.VMEM((2, members, members), jnp.float32),
             pltpu.VMEM((2, 1, members), jnp.float32),
         ],
-        cost_estimate=estimate(5 * flops, *inputs, shape),
+        cost_estimate=estimate(5 * flops, *inputs[:-1], shape),
         compiler_params=pltpu.CompilerParams(vmem_limit_bytes=VMEM_LIMIT),
     )(*inputs)
 
@@ -265,45 +274,50 @@
     def exchange(x):
         return lax.all_to_all(x, ("gx", "gy"), split_axis=0, concat_axis=0, tiled=True)
 
-    def section(group, begin):
+    def section(group, turn, begin):
         def pick(x):
             x = x.reshape(x.shape[0], levels, width, members)[:, :, begin : begin + SUB]
+            x = jnp.roll(x, -turn, axis=1)
             return x.reshape(x.shape[0], levels * SUB, members)
 
         return jnp.concatenate([pick(x) for x in group], axis=0)
 
-    packed = [
-        pack(background, nx, ny, q * width, width).reshape(members, lat, levels * width)
-        for q in range(number)
-    ]
-    groups, mixed = [], []
+    def halo_of(core):
+        up = shift(core[lat - HALO :], "gy", 1, False)
+        return up, shift(core[:HALO], "gy", -1, False)
+
+    def with_core(q):
+        return halos[q][0], cores[q], halos[q][1]
+
+    last = number - 1
+    transfers, cores, halos = [], [], []
     for q in range(number):
-        send = packed[q]
-        if q >= 3:
-            send, mixed[q - 3] = lax.optimization_barrier((send, mixed[q - 3]))
-        gathered = exchange(send)
-        core = jnp.transpose(gathered, (1, 2, 0))
-        up = shift(core[lat - HALO :], "gy", 1, False)
-        down = shift(core[:HALO], "gy", -1, False)
-        groups.append((up, core, down))
-        if q == 0:
-            after = shift(section(groups[0], 0), "gx", -1, True)
-        if q in range(1, number - 1):
-            table = tables[2 * q - 1 : 2 * q + 1]
-            mixed.append(analyse(True, (*groups[q - 1], *groups[q], table), levels))
-    q = number - 1
-    mixed[0], gathered, mixed[-1] = lax.optimization_barrier((mixed[0], gathered, mixed[-1]))
-    before = shift(section(groups[-1], width - SUB), "gx", 1, True)
-    table = tables[2 * q - 1 : 2 * q + 1]
-    mixed.append(analyse(True, (*groups[q - 1], *groups[q], table), levels))
-    table = jnp.stack([tables[-1], tables[0]])
-    mixed.append(analyse(False, (*groups[-1], *groups[0], after, before, table), levels))
-    chunks = []
+        send = pack(background, nx, ny, q, width).reshape(members, lat, levels * width)
+        if q >= 2:
+            send, halos[q - 2] = lax.optimization_barrier((send, halos[q - 2]))
+        transfers.append(exchange(send))
+        cores.append(jnp.transpose(transfers[q], (1, 2, 0)))
+        halos.append(halo_of(cores[q]))
+    after = shift(section(with_core(0), 0, 0), "gx", -1, True)
+    before = None
     for c in range(number):
-        back = jnp.transpose(mixed[c], (2, 0, 1))
-        if 0 < c < number - 1:
-            back, mixed[c + 1] = lax.optimization_barrier((back, mixed[c + 1]))
-        chunks.append(exchange(back).reshape(nx, ny, here, lat, levels * width))
+        table = tables[2 * c + 1 : 2 * c + 3] if c < last else jnp.stack([tables[-1], tables[0]])
+        inputs = (*with_core(c), *with_core((c + 1) % number))
+        if c == last:
+            inputs = (*inputs, after, before)
+        mixed = analyse(c, c < last, (*inputs, table, transfers[c + 2]), levels)
+        back = jnp.transpose(mixed, (2, 0, 1))
+        if c == 0:
+            back, halos[last - 1] = lax.optimization_barrier((back, halos[last - 1]))
+        if c == 1:
+            back, halos[last], after = lax.optimization_barrier((back, halos[last], after))
+            before = shift(section(with_core(last), last, width - SUB), "gx", 1, True)
+        if c == 2:
+            back, before = lax.optimization_barrier((back, before))
+        if c == 0:
+            back, transfers[last] = lax.optimization_barrier((back, transfers[last]))
+        transfers.append(exchange(back))
+    chunks = [t.reshape(nx, ny, here, lat, levels * width) for t in transfers[number:]]
     return unpack(chunks, background.shape)
 
 

time: 561 us -> 469 us (0.84)
  starting transfers between devices: 118 us -> 61.8 us
  waiting for transfers between devices: 232 us -> 199 us
    all_to_all x7, starting transfers between devices: 97.5 us -> 43.3 us  [exchange(): lax.all_to_all(x, ('gx', 'gy'), split_axis=0, concat_axis=0, tiled=True)]
    ppermute x10, waiting for transfers between devices: 56.5 us -> 33.8 us  [shift(): return lax.ppermute(x, axis, pairs)]
    all_to_all x7, waiting for transfers between devices: 175 us -> 165 us  [exchange(): lax.all_to_all(x, ('gx', 'gy'), split_axis=0, concat_axis=0, tiled=True)]
    pallas_call x0 -> x2, local copies, waits for them, and re-layouts: none -> 6.07 us  [analyse(): pl.pallas_call(functools.partial(pair_kernel, turn, inside), out_shape=sh...]
    unnamed x46 -> x62, local copies, waits for them, and re-layouts: 19 us -> 23.1 us
    slice x11 -> x17, local copies, waits for them, and re-layouts: 8.33 us -> 12.3 us  [the longest x4 8.18 us: halo_of(): return (up, shift(core[:HALO], 'gy', -1, False))]
  transfers between devices with their start and end apart: 17 -> 17, of which waited for: 10 -> 9; matrix products, arithmetic and copies ran while one was open for 7% -> 8% of each run, Pallas kernels for 13% -> 16%
where the time goes in v3:
time: 469 us; the launch traced here: 466 us
  waiting for transfers between devices  199 us (42%)
  Pallas kernels  91.5 us (20%)
  starting transfers between devices  61.8 us (13%)
  local copies, waits for them, and re-layouts  57.6 us (12%)
  blocking collectives  52.3 us (11%)
    all_to_all x7, waiting for transfers between devices, exchange(): lax.all_to_all(x, ('gx', 'gy'), split_axis=0, concat_axis=0, tiled=True)  165 us
    all_to_all x1, blocking collectives, exchange(): lax.all_to_all(x, ('gx', 'gy'), split_axis=0, concat_axis=0, tiled=True)  52.3 us
    pallas_call x4, Pallas kernels, analyse(): pl.pallas_call(functools.partial(pair_kernel, turn, inside), out_shape=sh...  50 us
    all_to_all x7, starting transfers between devices, exchange(): lax.all_to_all(x, ('gx', 'gy'), split_axis=0, concat_axis=0, tiled=True)  43.3 us
    ppermute x10, waiting for transfers between devices, shift(): return lax.ppermute(x, axis, pairs)  33.8 us
    pallas_call x4, Pallas kernels, pack(): pl.pallas_call(functools.partial(pack_kernel, ny, turn, width), out_shape...  31.7 us
    unnamed x62, local copies, waits for them, and re-layouts  23.1 us
    ppermute x10, starting transfers between devices, shift(): return lax.ppermute(x, axis, pairs)  18.5 us
  transfers between devices with their start and end apart: 17, of which 9 were waited for; matrix products, arithmetic and copies ran while one was open for 8% of the time, Pallas kernels for 16%

profile of v3, /device:TPU:0, one launch (start us, length us, event | category | flops | bytes accessed | tf_op | source)
XLA Modules:
  0.0 466.1 jit_solution(9540832612368363986)
XLA Ops:
  0.0 7.9 %shard_map.65 = f32[4,8,8,16,128]{4,3,2,1,0:T(8,128)} custom-call(f32[8,4,128,512]{3,2,1,0:T(8,128)} %source.7), custom_call_target="tpu_custom_call" | custom-call | bytes 10485760 | tf_op jit(solution)/shard_map/pallas_call | solution.py:181
  7.9 7.3 %all-to-all-start = ((f32[256,16,128]{2,1,0:T(8,128)}), f32[256,16,128]{2,1,0:T(8,128)S(1)}, u32[]{:S(2)}, u32[]{:S(2)}) async-start(f32[256,16,128]{2,1,0:T(8,128)} %bitcast.124), calls=%async_computation | async-start | bytes 4194304 | tf_op jit(solution)/shard_map/all_to_all | solution.py:275
  15.2 7.9 %shard_map.67 = f32[4,8,8,16,128]{4,3,2,1,0:T(8,128)} custom-call(f32[8,4,128,512]{3,2,1,0:T(8,128)} %source.7), custom_call_target="tpu_custom_call" | custom-call | bytes 10485760 | tf_op jit(solution)/shard_map/pallas_call | solution.py:181
  23.1 42.1 %all-to-all-done = f32[256,16,128]{2,1,0:T(8,128)S(1)} async-done(((f32[256,16,128]{2,1,0:T(8,128)}), f32[256,16,128]{2,1,0:T(8,128)S(1)}, u32[]{:S(2)}, u32[]{:S(2)}) %all-to-all-start) | async-done | bytes 2097184 | tf_op jit(solution)/shard_map/all_to_all | solution.py:275
  76.3 7.9 %shard_map.64 = f32[4,8,8,16,128]{4,3,2,1,0:T(8,128)} custom-call(f32[8,4,128,512]{3,2,1,0:T(8,128)} %source.7), custom_call_target="tpu_custom_call" | custom-call | bytes 10485760 | tf_op jit(solution)/shard_map/pallas_call | solution.py:181
  84.3 35.8 %all-to-all-done.1 = f32[256,16,128]{2,1,0:T(8,128)} async-done(((f32[256,16,128]{2,1,0:T(8,128)}), f32[256,16,128]{2,1,0:T(8,128)}, u32[]{:S(2)}, u32[]{:S(2)}) %all-to-all-start.1) | async-done | bytes 2097184 | tf_op jit(solution)/shard_map/all_to_all | solution.py:275
  120.0 6.8 %all-to-all-start.2 = ((f32[256,16,128]{2,1,0:T(8,128)}), f32[256,16,128]{2,1,0:T(8,128)S(1)}, u32[]{:S(2)}, u32[]{:S(2)}) async-start(f32[256,16,128]{2,1,0:T(8,128)} %bitcast.122), calls=%async_computation.2 | async-start | bytes 4194304 | tf_op jit(solution)/shard_map/all_to_all | solution.py:275
  135.6 7.9 %shard_map.66 = f32[4,8,8,16,128]{4,3,2,1,0:T(8,128)} custom-call(f32[8,4,128,512]{3,2,1,0:T(8,128)} %source.7), custom_call_target="tpu_custom_call" | custom-call | bytes 10485760 | tf_op jit(solution)/shard_map/pallas_call | solution.py:181
  144.3 32.5 %all-to-all-done.2.refs_7_ = f32[256,16,128]{2,1,0:T(8,128)S(1)} async-done(((f32[256,16,128]{2,1,0:T(8,128)}), f32[256,16,128]{2,1,0:T(8,128)S(1)}, u32[]{:S(2)}, u32[]{:S(2)}) %all-to-all-start.2) | async-done | bytes 2097184 | tf_op jit(solution)/shard_map/all_to_all | solution.py:275
  178.3 7.8 %all-to-all-start.3 = ((f32[256,16,128]{2,1,0:T(8,128)}), f32[256,16,128]{2,1,0:T(8,128)S(1)}, u32[]{:S(2)}, u32[]{:S(2)}) async-start(f32[256,16,128]{2,1,0:T(8,128)} %bitcast.121), calls=%async_computation.3 | async-start | bytes 4194304 | tf_op jit(solution)/shard_map/all_to_all | solution.py:275
  203.9 12.3 %shard_map.68 = f32[16,128,256]{2,1,0:T(8,128)S(1)} custom-call(f32[4,128,256]{2,1,0:T(8,128)S(1)} %collective-permute-done.refs_0_.refs_3_, f32[16,128,256]{2,1,0:T(8,128)S(1)} %bitcast.102, f32[4,128,256]{2,1,0:T(8,128)S(1)} %collective-permute-done.1.refs_2_.refs_5_, f32[4,128,256]{2,1,0:T(8,128)S(1)} %copy-done.23, f32[16,128,256]{2,1,0:T(8,128)S(1)} %bitcast.105, ...), custom_call_target="tpu_custom_call" | custom-call | flops 25165824000 | bytes 8425472 | tf_op jit(solution)/shard_map/pallas_call | solution.py:211
  220.7 15.5 %all-to-all-done.3.refs_7_ = f32[256,16,128]{2,1,0:T(8,128)S(1)} async-done(((f32[256,16,128]{2,1,0:T(8,128)}), f32[256,16,128]{2,1,0:T(8,128)S(1)}, u32[]{:S(2)}, u32[]{:S(2)}) %all-to-all-start.3) | async-done | bytes 2097184 | tf_op jit(solution)/shard_map/all_to_all | solution.py:275
  236.1 7.4 %all-to-all-start.4 = ((f32[256,16,128]{2,1,0:T(8,128)}), f32[256,16,128]{2,1,0:T(8,128)}, u32[]{:S(2)}, u32[]{:S(2)}) async-start(f32[256,16,128]{2,1,0:T(8,128)} %bitcast.125), calls=%async_computation.4 | async-start | bytes 4194304 | tf_op jit(solution)/shard_map/all_to_all | solution.py:275
  258.2 12.7 %shard_map.69 = f32[16,128,256]{2,1,0:T(8,128)S(1)} custom-call(f32[4,128,256]{2,1,0:T(8,128)S(1)} %copy-done.24, f32[16,128,256]{2,1,0:T(8,128)S(1)} %bitcast.106, f32[4,128,256]{2,1,0:T(8,128)} %collective-permute-done.3.refs_5_.refs_2_, f32[4,128,256]{2,1,0:T(8,128)} %collective-permute-done.4.refs_3_.refs_0_, f32[16,128,256]{2,1,0:T(8,128)S(1)} %bitcast.108, ...), custom_call_target="tpu_custom_call" | custom-call | flops 25165824000 | bytes 8425472 | tf_op jit(solution)/shard_map/pallas_call | solution.py:211
  275.4 8.6 %collective-permute-done.8.refs_6_ = f32[24,32,256]{2,1,0:T(8,128)} collective-permute-done((f32[24,32,256]{2,1,0:T(8,128)}, f32[24,32,256]{2,1,0:T(8,128)}, u32[]{:S(2)}, u32[]{:S(2)}) %collective-permute-start.8) | collective-permute-done | bytes 786464 | tf_op jit(solution)/shard_map/ppermute | solution.py:258
  284.0 9.4 %all-to-all-done.4.refs_7_ = f32[256,16,128]{2,1,0:T(8,128)} async-done(((f32[256,16,128]{2,1,0:T(8,128)}), f32[256,16,128]{2,1,0:T(8,128)}, u32[]{:S(2)}, u32[]{:S(2)}) %all-to-all-start.4) | async-done | bytes 2097184 | tf_op jit(solution)/shard_map/all_to_all | solution.py:275
  293.4 6.9 %all-to-all-start.5 = ((f32[256,16,128]{2,1,0:T(8,128)}), f32[256,16,128]{2,1,0:T(8,128)S(1)}, u32[]{:S(2)}, u32[]{:S(2)}) async-start(f32[256,16,128]{2,1,0:T(8,128)} %bitcast.126), calls=%async_computation.5 | async-start | bytes 4194304 | tf_op jit(solution)/shard_map/all_to_all | solution.py:275
  304.9 12.5 %shard_map.70 = f32[16,128,256]{2,1,0:T(8,128)S(1)} custom-call(f32[4,128,256]{2,1,0:T(8,128)} %collective-permute-done.4.refs_3_.refs_0_, f32[16,128,256]{2,1,0:T(8,128)S(1)} %bitcast.109, f32[4,128,256]{2,1,0:T(8,128)} %collective-permute-done.5.refs_5_.refs_2_, f32[4,128,256]{2,1,0:T(8,128)S(1)} %collective-permute-done.6.refs_3_.refs_0_, ...), custom_call_target="tpu_custom_call" | custom-call | flops 25165824000 | bytes 8425472 | tf_op jit(solution)/shard_map/pallas_call | solution.py:211
  318.8 25.2 %collective-permute-done.9.refs_7_ = f32[24,32,256]{2,1,0:T(8,128)S(1)} collective-permute-done((f32[24,32,256]{2,1,0:T(8,128)S(1)}, f32[24,32,256]{2,1,0:T(8,128)S(1)}, u32[]{:S(2)}, u32[]{:S(2)}) %collective-permute-start.9) | collective-permute-done | bytes 786464 | tf_op jit(solution)/shard_map/ppermute | solution.py:258
  350.4 3.6 all-to-all-start.6
  360.6 12.5 %shard_map.71 = f32[16,128,256]{2,1,0:T(8,128)S(1)} custom-call(f32[4,128,256]{2,1,0:T(8,128)S(1)} %collective-permute-done.6.refs_3_.refs_0_, f32[16,128,256]{2,1,0:T(8,128)S(1)} %bitcast.99, f32[4,128,256]{2,1,0:T(8,128)S(1)} %collective-permute-done.7.refs_5_.refs_2_, f32[4,128,256]{2,1,0:T(8,128)S(1)} %copy-done.17, f32[16,128,256]{2,1,0:T(8,128)S(1)} %bitcast.103, ...), custom_call_target="tpu_custom_call" | custom-call | flops 25165824000 | bytes 9998336 | tf_op jit(solution)/shard_map/pallas_call | solution.py:211
  376.6 27.3 %all-to-all-done.6 = f32[256,16,128]{2,1,0:T(8,128)} async-done(((f32[256,16,128]{2,1,0:T(8,128)}), f32[256,16,128]{2,1,0:T(8,128)}, u32[]{:S(2)}, u32[]{:S(2)}) %all-to-all-start.6) | async-done | bytes 2097184 | tf_op jit(solution)/shard_map/all_to_all | solution.py:275
  404.0 52.3 %all_to_all.40 = f32[256,16,128]{2,1,0:T(8,128)} all-to-all(f32[256,16,128]{2,1,0:T(8,128)S(1)} %copy.49), channel_id=1, replica_groups=mesh['gx'=4,'gy'=8] {'gx','gy'}, dimensions={0} | all-to-all | bytes 4194304 | tf_op jit(solution)/shard_map/all_to_all | solution.py:275
  456.3 9.8 %shard_map.72 = f32[8,4,128,512]{3,2,1,0:T(8,128)} custom-call(f32[4,8,8,16,128]{4,3,2,1,0:T(8,128)} %bitcast.18.refs_0_, f32[4,8,8,16,128]{4,3,2,1,0:T(8,128)} %bitcast.94, f32[4,8,8,16,128]{4,3,2,1,0:T(8,128)} %bitcast.38.refs_2_, f32[4,8,8,16,128]{4,3,2,1,0:T(8,128)} %bitcast.127), custom_call_target="tpu_custom_call" | custom-call | bytes 16777216 | tf_op jit(solution)/shard_map/pallas_call | solution.py:194
  (120 shorter events, 85.5 us)
Async XLA Ops:
  7.9 57.4 %all-to-all-start = ((f32[256,16,128]{2,1,0:T(8,128)}), f32[256,16,128]{2,1,0:T(8,128)S(1)}, u32[]{:S(2)}, u32[]{:S(2)}) async-start(f32[256,16,128]{2,1,0:T(8,128)} %bitcast.124), calls=%async_computation | async-start | bytes 4194304 | tf_op jit(solution)/shard_map/all_to_all | solution.py:275
  66.5 53.5 %all-to-all-start.1 = ((f32[256,16,128]{2,1,0:T(8,128)}), f32[256,16,128]{2,1,0:T(8,128)}, u32[]{:S(2)}, u32[]{:S(2)}) async-start(f32[256,16,128]{2,1,0:T(8,128)} %bitcast.123), calls=%async_computation.1 | async-start | bytes 4194304 | tf_op jit(solution)/shard_map/all_to_all | solution.py:275
  73.0 11.2 %collective-permute-start = (f32[4,128,256]{2,1,0:T(8,128)}, f32[4,128,256]{2,1,0:T(8,128)S(1)}, u32[]{:S(2)}, u32[]{:S(2)}) collective-permute-start(f32[4,128,256]{2,1,0:T(8,128)} %get-tuple-element.48), channel_id=1, source_target_pairs={{0,1},{1,2},{2,3},{3,4},{4,5},{5,6},{6,7},{8,9},{9,10},{10,11},{11... | collective-permute-start | bytes 1572872 | tf_op jit(solution)/shard_map/ppermute | solution.py:258
  75.0 9.2 %collective-permute-start.1 = (f32[4,128,256]{2,1,0:T(8,128)S(1)}, f32[4,128,256]{2,1,0:T(8,128)S(1)}, u32[]{:S(2)}, u32[]{:S(2)}) collective-permute-start(f32[4,128,256]{2,1,0:T(8,128)S(1)} %get-tuple-element.47), channel_id=1, source_target_pairs={{1,0},{2,1},{3,2},{4,3},{5,4},{6,5},{7,6},{9,8},{10,9},{11,10},{12... | collective-permute-start | bytes 1572872 | tf_op jit(solution)/shard_map/ppermute | solution.py:258
  84.2 160.5 %copy-start.16 = (f32[4,128,256]{2,1,0:T(8,128)}, f32[4,128,256]{2,1,0:T(8,128)S(1)}, u32[]{:S(2)}) copy-start(f32[4,128,256]{2,1,0:T(8,128)S(1)} %collective-permute-done.refs_0_.refs_3_) | copy-start | bytes 1572868
  84.3 160.5 %copy-start.18 = (f32[4,128,256]{2,1,0:T(8,128)}, f32[4,128,256]{2,1,0:T(8,128)S(1)}, u32[]{:S(2)}) copy-start(f32[4,128,256]{2,1,0:T(8,128)S(1)} %collective-permute-done.1.refs_2_.refs_5_) | copy-start | bytes 1572868
  120.0 56.8 %all-to-all-start.2 = ((f32[256,16,128]{2,1,0:T(8,128)}), f32[256,16,128]{2,1,0:T(8,128)S(1)}, u32[]{:S(2)}, u32[]{:S(2)}) async-start(f32[256,16,128]{2,1,0:T(8,128)} %bitcast.122), calls=%async_computation.2 | async-start | bytes 4194304 | tf_op jit(solution)/shard_map/all_to_all | solution.py:275
  132.1 11.4 %collective-permute-start.2 = (f32[4,128,256]{2,1,0:T(8,128)}, f32[4,128,256]{2,1,0:T(8,128)S(1)}, u32[]{:S(2)}, u32[]{:S(2)}) collective-permute-start(f32[4,128,256]{2,1,0:T(8,128)} %get-tuple-element.46), channel_id=1, source_target_pairs={{0,1},{1,2},{2,3},{3,4},{4,5},{5,6},{6,7},{8,9},{9,10},{10,11},{11... | collective-permute-start | bytes 1572872 | tf_op jit(solution)/shard_map/ppermute | solution.py:258
  134.3 10.1 %collective-permute-start.3 = (f32[4,128,256]{2,1,0:T(8,128)}, f32[4,128,256]{2,1,0:T(8,128)}, u32[]{:S(2)}, u32[]{:S(2)}) collective-permute-start(f32[4,128,256]{2,1,0:T(8,128)} %get-tuple-element.45), channel_id=1, source_target_pairs={{1,0},{2,1},{3,2},{4,3},{5,4},{6,5},{7,6},{9,8},{10,9},{11,10},{12... | collective-permute-start | bytes 1572872 | tf_op jit(solution)/shard_map/ppermute | solution.py:258
  144.3 41.8 %copy-start.29 = (s32[1,8]{1,0:T(1,128)S(1)}, s32[1,8]{1,0:T(1,128)}, u32[]{:S(2)}) copy-start(s32[1,8]{1,0:T(1,128)} %param.9) | copy-start | bytes 100
  144.3 41.8 %copy-start.26 = (s32[1,8,1024]{2,1,0:T(8,128)S(1)}, s32[1,8,1024]{2,1,0:T(8,128)}, u32[]{:S(2)}) copy-start(s32[1,8,1024]{2,1,0:T(8,128)} %param.7) | copy-start | bytes 98308
  144.3 41.9 %copy-start.27 = (f32[1,8,1024]{2,1,0:T(8,128)S(1)}, f32[1,8,1024]{2,1,0:T(8,128)}, u32[]{:S(2)}) copy-start(f32[1,8,1024]{2,1,0:T(8,128)} %param.10) | copy-start | bytes 98308
  144.3 41.9 %copy-start.28 = (f32[1,8,1024]{2,1,0:T(8,128)S(1)}, f32[1,8,1024]{2,1,0:T(8,128)}, u32[]{:S(2)}) copy-start(f32[1,8,1024]{2,1,0:T(8,128)} %param.11) | copy-start | bytes 98308
  144.3 41.9 %copy-start.30 = (s32[1,8]{1,0:T(1,128)S(1)}, s32[1,8]{1,0:T(1,128)}, u32[]{:S(2)}) copy-start(s32[1,8]{1,0:T(1,128)} %param.8) | copy-start | bytes 100
  178.3 57.9 %all-to-all-start.3 = ((f32[256,16,128]{2,1,0:T(8,128)}), f32[256,16,128]{2,1,0:T(8,128)S(1)}, u32[]{:S(2)}, u32[]{:S(2)}) async-start(f32[256,16,128]{2,1,0:T(8,128)} %bitcast.121), calls=%async_computation.3 | async-start | bytes 4194304 | tf_op jit(solution)/shard_map/all_to_all | solution.py:275
  195.4 25.3 %collective-permute-start.4 = (f32[4,128,256]{2,1,0:T(8,128)}, f32[4,128,256]{2,1,0:T(8,128)}, u32[]{:S(2)}, u32[]{:S(2)}) collective-permute-start(f32[4,128,256]{2,1,0:T(8,128)} %get-tuple-element.44), channel_id=1, source_target_pairs={{0,1},{1,2},{2,3},{3,4},{4,5},{5,6},{6,7},{8,9},{9,10},{10,11},{11... | collective-permute-start | bytes 1572872 | tf_op jit(solution)/shard_map/ppermute | solution.py:258
  198.4 22.3 %collective-permute-start.5 = (f32[4,128,256]{2,1,0:T(8,128)}, f32[4,128,256]{2,1,0:T(8,128)}, u32[]{:S(2)}, u32[]{:S(2)}) collective-permute-start(f32[4,128,256]{2,1,0:T(8,128)} %get-tuple-element.43), channel_id=1, source_target_pairs={{1,0},{2,1},{3,2},{4,3},{5,4},{6,5},{7,6},{9,8},{10,9},{11,10},{12... | collective-permute-start | bytes 1572872 | tf_op jit(solution)/shard_map/ppermute | solution.py:258
  236.1 57.2 %all-to-all-start.4 = ((f32[256,16,128]{2,1,0:T(8,128)}), f32[256,16,128]{2,1,0:T(8,128)}, u32[]{:S(2)}, u32[]{:S(2)}) async-start(f32[256,16,128]{2,1,0:T(8,128)} %bitcast.125), calls=%async_computation.4 | async-start | bytes 4194304 | tf_op jit(solution)/shard_map/all_to_all | solution.py:275
  245.8 38.2 %collective-permute-start.8 = (f32[24,32,256]{2,1,0:T(8,128)}, f32[24,32,256]{2,1,0:T(8,128)}, u32[]{:S(2)}, u32[]{:S(2)}) collective-permute-start(f32[24,32,256]{2,1,0:T(8,128)} %pad_maximum_fusion), channel_id=1, source_target_pairs={{0,24},{8,0},{16,8},{24,16},{1,25},{9,1},{17,9},{25,17},{2,26},{10... | collective-permute-start | bytes 2359304 | tf_op jit(solution)/shard_map/ppermute | solution.py:258
  252.5 31.5 %collective-permute-start.6 = (f32[4,128,256]{2,1,0:T(8,128)}, f32[4,128,256]{2,1,0:T(8,128)S(1)}, u32[]{:S(2)}, u32[]{:S(2)}) collective-permute-start(f32[4,128,256]{2,1,0:T(8,128)} %get-tuple-element.42), channel_id=1, source_target_pairs={{0,1},{1,2},{2,3},{3,4},{4,5},{5,6},{6,7},{8,9},{9,10},{10,11},{11... | collective-permute-start | bytes 1572872 | tf_op jit(solution)/shard_map/ppermute | solution.py:258
  254.3 29.7 %collective-permute-start.7 = (f32[4,128,256]{2,1,0:T(8,128)}, f32[4,128,256]{2,1,0:T(8,128)S(1)}, u32[]{:S(2)}, u32[]{:S(2)}) collective-permute-start(f32[4,128,256]{2,1,0:T(8,128)} %get-tuple-element.41), channel_id=1, source_target_pairs={{1,0},{2,1},{3,2},{4,3},{5,4},{6,5},{7,6},{9,8},{10,9},{11,10},{12... | collective-permute-start | bytes 1572872 | tf_op jit(solution)/shard_map/ppermute | solution.py:258
  293.4 57.0 %all-to-all-start.5 = ((f32[256,16,128]{2,1,0:T(8,128)}), f32[256,16,128]{2,1,0:T(8,128)S(1)}, u32[]{:S(2)}, u32[]{:S(2)}) async-start(f32[256,16,128]{2,1,0:T(8,128)} %bitcast.126), calls=%async_computation.5 | async-start | bytes 4194304 | tf_op jit(solution)/shard_map/all_to_all | solution.py:275
  302.9 41.1 %collective-permute-start.9 = (f32[24,32,256]{2,1,0:T(8,128)S(1)}, f32[24,32,256]{2,1,0:T(8,128)S(1)}, u32[]{:S(2)}, u32[]{:S(2)}) collective-permute-start(f32[24,32,256]{2,1,0:T(8,128)S(1)} %pad_maximum_fusion.1), channel_id=1, source_target_pairs={{0,8},{8,16},{16,24},{24,0},{1,9},{9,17},{17,25},{25,1},{2,10},{10... | collective-permute-start | bytes 2359304 | tf_op jit(solution)/shard_map/ppermute | solution.py:258
  350.4 53.6 %all-to-all-start.6 = ((f32[256,16,128]{2,1,0:T(8,128)}), f32[256,16,128]{2,1,0:T(8,128)}, u32[]{:S(2)}, u32[]{:S(2)}) async-start(f32[256,16,128]{2,1,0:T(8,128)} %copy.46), calls=%async_computation.6 | async-start | bytes 4194304 | tf_op jit(solution)/shard_map/all_to_all | solution.py:275
  (24 other events, 59.3 us)

commit v4 on v3

--- a/solution.py
+++ b/solution.py
@@ -276,11 +276,16 @@
 
     def section(group, turn, begin):
         def pick(x):
-            x = x.reshape(x.shape[0], levels, width, members)[:, :, begin : begin + SUB]
+            x = x.reshape(x.shape[0], levels, width, members)[:, :, begin : begin + HALO]
             x = jnp.roll(x, -turn, axis=1)
-            return x.reshape(x.shape[0], levels * SUB, members)
+            return x.reshape(x.shape[0], levels * HALO, members)
 
         return jnp.concatenate([pick(x) for x in group], axis=0)
+
+    def widen(x, low):
+        x = x.reshape(x.shape[0], levels, HALO, members)
+        x = jnp.pad(x, ((0, 0), (0, 0), (low, SUB - HALO - low), (0, 0)))
+        return x.reshape(x.shape[0], levels * SUB, members)
 
     def halo_of(core):
         up = shift(core[lat - HALO :], "gy", 1, False)
@@ -304,14 +309,14 @@
         table = tables[2 * c + 1 : 2 * c + 3] if c < last else jnp.stack([tables[-1], tables[0]])
         inputs = (*with_core(c), *with_core((c + 1) % number))
         if c == last:
-            inputs = (*inputs, after, before)
+            inputs = (*inputs, widen(after, 0), widen(before, SUB - HALO))
         mixed = analyse(c, c < last, (*inputs, table, transfers[c + 2]), levels)
         back = jnp.transpose(mixed, (2, 0, 1))
         if c == 0:
             back, halos[last - 1] = lax.optimization_barrier((back, halos[last - 1]))
         if c == 1:
             back, halos[last], after = lax.optimization_barrier((back, halos[last], after))
-            before = shift(section(with_core(last), last, width - SUB), "gx", 1, True)
+            before = shift(section(with_core(last), last, width - HALO), "gx", 1, True)
         if c == 2:
             back, before = lax.optimization_barrier((back, before))
         if c == 0:

time: 469 us -> 469 us (level)
  waiting for transfers between devices: 199 us -> 179 us
  local copies, waits for them, and re-layouts: 57.6 us -> 70.5 us
  starting transfers between devices: 61.8 us -> 66.5 us
    ppermute x10, waiting for transfers between devices: 33.8 us -> 1.33 us  [shift(): return lax.ppermute(x, axis, pairs)]
    all_to_all x7, waiting for transfers between devices: 165 us -> 177 us  [exchange(): lax.all_to_all(x, ('gx', 'gy'), split_axis=0, concat_axis=0, tiled=True)]
    reshape x2 -> x9, local copies, waits for them, and re-layouts: 1.11 us -> 11.1 us  [the longest x6 5.92 us: pick(): return x.reshape(x.shape[0], levels * HALO, members)]
    ppermute x10, starting transfers between devices: 18.5 us -> 23.4 us  [shift(): return lax.ppermute(x, axis, pairs)]
    unnamed x62 -> x60, local copies, waits for them, and re-layouts: 23.1 us -> 23.7 us
  transfers between devices with their start and end apart: 17 -> 17, of which waited for: 9 -> 8; matrix products, arithmetic and copies ran while one was open for 8% -> 11% of each run, Pallas kernels for 16% -> 16%
where the time goes in v4:
time: 469 us; the launch traced here: 466 us
  waiting for transfers between devices  179 us (38%)
  Pallas kernels  90.3 us (19%)
  local copies, waits for them, and re-layouts  70.5 us (15%)
  starting transfers between devices  66.5 us (14%)
  blocking collectives  52.3 us (11%)
  other arithmetic  4.79 us (1%)
    all_to_all x7, waiting for transfers between devices, exchange(): lax.all_to_all(x, ('gx', 'gy'), split_axis=0, concat_axis=0, tiled=True)  177 us
    all_to_all x1, blocking collectives, exchange(): lax.all_to_all(x, ('gx', 'gy'), split_axis=0, concat_axis=0, tiled=True)  52.3 us
    pallas_call x4, Pallas kernels, analyse(): pl.pallas_call(functools.partial(pair_kernel, turn, inside), out_shape=sh...  48.9 us
    all_to_all x7, starting transfers between devices, exchange(): lax.all_to_all(x, ('gx', 'gy'), split_axis=0, concat_axis=0, tiled=True)  43.1 us
    pallas_call x4, Pallas kernels, pack(): pl.pallas_call(functools.partial(pack_kernel, ny, turn, width), out_shape...  31.6 us
    unnamed x60, local copies, waits for them, and re-layouts  23.7 us
    ppermute x10, starting transfers between devices, shift(): return lax.ppermute(x, axis, pairs)  23.4 us
    pallas_call x1, Pallas kernels, unpack(): pl.pallas_call(unpack_kernel, out_shape=jax.ShapeDtypeStruct(shape, chunk...  9.83 us
  transfers between devices with their start and end apart: 17, of which 8 were waited for; matrix products, arithmetic and copies ran while one was open for 11% of the time, Pallas kernels for 16%

profile of v4, /device:TPU:0, one launch (start us, length us, event | category | flops | bytes accessed | tf_op | source)
XLA Modules:
  0.0 465.6 jit_solution(9971810201037127927)
XLA Ops:
  0.0 7.9 %shard_map.65 = f32[4,8,8,16,128]{4,3,2,1,0:T(8,128)} custom-call(f32[8,4,128,512]{3,2,1,0:T(8,128)} %source.7), custom_call_target="tpu_custom_call" | custom-call | bytes 10485760 | tf_op jit(solution)/shard_map/pallas_call | solution.py:181
  7.9 7.3 %all-to-all-start = ((f32[256,16,128]{2,1,0:T(8,128)}), f32[256,16,128]{2,1,0:T(8,128)S(1)}, u32[]{:S(2)}, u32[]{:S(2)}) async-start(f32[256,16,128]{2,1,0:T(8,128)} %bitcast.116), calls=%async_computation | async-start | bytes 4194304 | tf_op jit(solution)/shard_map/all_to_all | solution.py:275
  15.2 7.9 %shard_map.67 = f32[4,8,8,16,128]{4,3,2,1,0:T(8,128)} custom-call(f32[8,4,128,512]{3,2,1,0:T(8,128)} %source.7), custom_call_target="tpu_custom_call" | custom-call | bytes 10485760 | tf_op jit(solution)/shard_map/pallas_call | solution.py:181
  23.1 42.1 %all-to-all-done = f32[256,16,128]{2,1,0:T(8,128)S(1)} async-done(((f32[256,16,128]{2,1,0:T(8,128)}), f32[256,16,128]{2,1,0:T(8,128)S(1)}, u32[]{:S(2)}, u32[]{:S(2)}) %all-to-all-start) | async-done | bytes 2097184 | tf_op jit(solution)/shard_map/all_to_all | solution.py:275
  77.4 7.9 %shard_map.64 = f32[4,8,8,16,128]{4,3,2,1,0:T(8,128)} custom-call(f32[8,4,128,512]{3,2,1,0:T(8,128)} %source.7), custom_call_target="tpu_custom_call" | custom-call | bytes 10485760 | tf_op jit(solution)/shard_map/pallas_call | solution.py:181
  85.3 34.7 %all-to-all-done.1 = f32[256,16,128]{2,1,0:T(8,128)} async-done(((f32[256,16,128]{2,1,0:T(8,128)}), f32[256,16,128]{2,1,0:T(8,128)}, u32[]{:S(2)}, u32[]{:S(2)}) %all-to-all-start.1) | async-done | bytes 2097184 | tf_op jit(solution)/shard_map/all_to_all | solution.py:275
  120.0 6.8 %all-to-all-start.2 = ((f32[256,16,128]{2,1,0:T(8,128)}), f32[256,16,128]{2,1,0:T(8,128)S(1)}, u32[]{:S(2)}, u32[]{:S(2)}) async-start(f32[256,16,128]{2,1,0:T(8,128)} %bitcast.114), calls=%async_computation.2 | async-start | bytes 4194304 | tf_op jit(solution)/shard_map/all_to_all | solution.py:275
  133.4 3.8 collective-permute-start.2
  137.2 7.9 %shard_map.66 = f32[4,8,8,16,128]{4,3,2,1,0:T(8,128)} custom-call(f32[8,4,128,512]{3,2,1,0:T(8,128)} %source.7), custom_call_target="tpu_custom_call" | custom-call | bytes 10485760 | tf_op jit(solution)/shard_map/pallas_call | solution.py:181
  146.0 30.9 %all-to-all-done.2.refs_7_ = f32[256,16,128]{2,1,0:T(8,128)S(1)} async-done(((f32[256,16,128]{2,1,0:T(8,128)}), f32[256,16,128]{2,1,0:T(8,128)S(1)}, u32[]{:S(2)}, u32[]{:S(2)}) %all-to-all-start.2) | async-done | bytes 2097184 | tf_op jit(solution)/shard_map/all_to_all | solution.py:275
  178.2 7.4 %all-to-all-start.3 = ((f32[256,16,128]{2,1,0:T(8,128)}), f32[256,16,128]{2,1,0:T(8,128)S(1)}, u32[]{:S(2)}, u32[]{:S(2)}) async-start(f32[256,16,128]{2,1,0:T(8,128)} %bitcast.113), calls=%async_computation.3 | async-start | bytes 4194304 | tf_op jit(solution)/shard_map/all_to_all | solution.py:275
  195.5 3.9 collective-permute-start.4
  203.6 12.3 %shard_map.68 = f32[16,128,256]{2,1,0:T(8,128)S(1)} custom-call(f32[4,128,256]{2,1,0:T(8,128)S(1)} %collective-permute-done.refs_0_.refs_3_, f32[16,128,256]{2,1,0:T(8,128)S(1)} %bitcast.89, f32[4,128,256]{2,1,0:T(8,128)S(1)} %collective-permute-done.1.refs_2_.refs_5_, f32[4,128,256]{2,1,0:T(8,128)} %collective-permute-done.2.refs_3_.refs_0_, ...), custom_call_target="tpu_custom_call" | custom-call | flops 25165824000 | bytes 8425472 | tf_op jit(solution)/shard_map/pallas_call | solution.py:211
  220.3 15.3 %all-to-all-done.3.refs_7_ = f32[256,16,128]{2,1,0:T(8,128)S(1)} async-done(((f32[256,16,128]{2,1,0:T(8,128)}), f32[256,16,128]{2,1,0:T(8,128)S(1)}, u32[]{:S(2)}, u32[]{:S(2)}) %all-to-all-start.3) | async-done | bytes 2097184 | tf_op jit(solution)/shard_map/all_to_all | solution.py:275
  235.7 7.4 %all-to-all-start.4 = ((f32[256,16,128]{2,1,0:T(8,128)}), f32[256,16,128]{2,1,0:T(8,128)}, u32[]{:S(2)}, u32[]{:S(2)}) async-start(f32[256,16,128]{2,1,0:T(8,128)} %bitcast.117), calls=%async_computation.4 | async-start | bytes 4194304 | tf_op jit(solution)/shard_map/all_to_all | solution.py:275
  262.0 12.7 %shard_map.69 = f32[16,128,256]{2,1,0:T(8,128)S(1)} custom-call(f32[4,128,256]{2,1,0:T(8,128)} %collective-permute-done.2.refs_3_.refs_0_, f32[16,128,256]{2,1,0:T(8,128)S(1)} %bitcast.101, f32[4,128,256]{2,1,0:T(8,128)S(1)} %copy-done.22, f32[4,128,256]{2,1,0:T(8,128)} %collective-permute-done.4.refs_3_.refs_0_, f32[16,128,256]{2,1,0:T(8,128)S(1)} %bitcast.97, ...), custom_call_target="tpu_custom_call" | custom-call | flops 25165824000 | bytes 8425472 | tf_op jit(solution)/shard_map/pallas_call | solution.py:211
  279.3 13.6 %all-to-all-done.4.refs_7_ = f32[256,16,128]{2,1,0:T(8,128)} async-done(((f32[256,16,128]{2,1,0:T(8,128)}), f32[256,16,128]{2,1,0:T(8,128)}, u32[]{:S(2)}, u32[]{:S(2)}) %all-to-all-start.4) | async-done | bytes 2097184 | tf_op jit(solution)/shard_map/all_to_all | solution.py:275
  292.9 6.9 %all-to-all-start.5 = ((f32[256,16,128]{2,1,0:T(8,128)}), f32[256,16,128]{2,1,0:T(8,128)S(1)}, u32[]{:S(2)}, u32[]{:S(2)}) async-start(f32[256,16,128]{2,1,0:T(8,128)} %bitcast.118), calls=%async_computation.5 | async-start | bytes 4194304 | tf_op jit(solution)/shard_map/all_to_all | solution.py:275
  315.4 12.5 %shard_map.70 = f32[16,128,256]{2,1,0:T(8,128)S(1)} custom-call(f32[4,128,256]{2,1,0:T(8,128)} %collective-permute-done.4.refs_3_.refs_0_, f32[16,128,256]{2,1,0:T(8,128)S(1)} %bitcast.98, f32[4,128,256]{2,1,0:T(8,128)} %collective-permute-done.5.refs_5_.refs_2_, f32[4,128,256]{2,1,0:T(8,128)S(1)} %collective-permute-done.6.refs_3_.refs_0_, ...), custom_call_target="tpu_custom_call" | custom-call | flops 25165824000 | bytes 8425472 | tf_op jit(solution)/shard_map/pallas_call | solution.py:211
  333.6 16.2 %all-to-all-done.5.refs_9_ = f32[256,16,128]{2,1,0:T(8,128)S(1)} async-done(((f32[256,16,128]{2,1,0:T(8,128)}), f32[256,16,128]{2,1,0:T(8,128)S(1)}, u32[]{:S(2)}, u32[]{:S(2)}) %all-to-all-start.5) | async-done | bytes 2097184 | tf_op jit(solution)/shard_map/all_to_all | solution.py:275
  363.9 11.3 %shard_map.71 = f32[16,128,256]{2,1,0:T(8,128)S(1)} custom-call(f32[4,128,256]{2,1,0:T(8,128)S(1)} %collective-permute-done.6.refs_3_.refs_0_, f32[16,128,256]{2,1,0:T(8,128)S(1)} %bitcast.95, f32[4,128,256]{2,1,0:T(8,128)S(1)} %collective-permute-done.7.refs_5_.refs_2_, f32[4,128,256]{2,1,0:T(8,128)S(1)} %copy-done.19, f32[16,128,256]{2,1,0:T(8,128)S(1)} %bitcast.90, ...), custom_call_target="tpu_custom_call" | custom-call | flops 25165824000 | bytes 9998336 | tf_op jit(solution)/shard_map/pallas_call | solution.py:211
  378.8 24.6 %all-to-all-done.6 = f32[256,16,128]{2,1,0:T(8,128)} async-done(((f32[256,16,128]{2,1,0:T(8,128)}), f32[256,16,128]{2,1,0:T(8,128)}, u32[]{:S(2)}, u32[]{:S(2)}) %all-to-all-start.6) | async-done | bytes 2097184 | tf_op jit(solution)/shard_map/all_to_all | solution.py:275
  403.4 52.3 %all_to_all.40 = f32[256,16,128]{2,1,0:T(8,128)} all-to-all(f32[256,16,128]{2,1,0:T(8,128)S(1)} %copy.49), channel_id=1, replica_groups=mesh['gx'=4,'gy'=8] {'gx','gy'}, dimensions={0} | all-to-all | bytes 4194304 | tf_op jit(solution)/shard_map/all_to_all | solution.py:275
  455.7 9.8 %shard_map.72 = f32[8,4,128,512]{3,2,1,0:T(8,128)} custom-call(f32[4,8,8,16,128]{4,3,2,1,0:T(8,128)} %bitcast.18.refs_0_, f32[4,8,8,16,128]{4,3,2,1,0:T(8,128)} %bitcast.86, f32[4,8,8,16,128]{4,3,2,1,0:T(8,128)} %bitcast.32.refs_2_, f32[4,8,8,16,128]{4,3,2,1,0:T(8,128)} %bitcast.119), custom_call_target="tpu_custom_call" | custom-call | bytes 16777216 | tf_op jit(solution)/shard_map/pallas_call | solution.py:194
  (128 shorter events, 101.6 us)
Async XLA Ops:
  7.9 57.4 %all-to-all-start = ((f32[256,16,128]{2,1,0:T(8,128)}), f32[256,16,128]{2,1,0:T(8,128)S(1)}, u32[]{:S(2)}, u32[]{:S(2)}) async-start(f32[256,16,128]{2,1,0:T(8,128)} %bitcast.116), calls=%async_computation | async-start | bytes 4194304 | tf_op jit(solution)/shard_map/all_to_all | solution.py:275
  66.5 53.5 %all-to-all-start.1 = ((f32[256,16,128]{2,1,0:T(8,128)}), f32[256,16,128]{2,1,0:T(8,128)}, u32[]{:S(2)}, u32[]{:S(2)}) async-start(f32[256,16,128]{2,1,0:T(8,128)} %bitcast.115), calls=%async_computation.1 | async-start | bytes 4194304 | tf_op jit(solution)/shard_map/all_to_all | solution.py:275
  73.0 12.3 %collective-permute-start.1 = (f32[4,128,256]{2,1,0:T(8,128)}, f32[4,128,256]{2,1,0:T(8,128)S(1)}, u32[]{:S(2)}, u32[]{:S(2)}) collective-permute-start(f32[4,128,256]{2,1,0:T(8,128)} %get-tuple-element.47), channel_id=1, source_target_pairs={{1,0},{2,1},{3,2},{4,3},{5,4},{6,5},{7,6},{9,8},{10,9},{11,10},{12... | collective-permute-start | bytes 1572872 | tf_op jit(solution)/shard_map/ppermute | solution.py:258
  74.3 11.0 %collective-permute-start = (f32[4,128,256]{2,1,0:T(8,128)S(1)}, f32[4,128,256]{2,1,0:T(8,128)S(1)}, u32[]{:S(2)}, u32[]{:S(2)}) collective-permute-start(f32[4,128,256]{2,1,0:T(8,128)S(1)} %get-tuple-element.48), channel_id=1, source_target_pairs={{0,1},{1,2},{2,3},{3,4},{4,5},{5,6},{6,7},{8,9},{9,10},{10,11},{11... | collective-permute-start | bytes 1572872 | tf_op jit(solution)/shard_map/ppermute | solution.py:258
  85.3 160.7 %copy-start.16 = (f32[4,128,256]{2,1,0:T(8,128)}, f32[4,128,256]{2,1,0:T(8,128)S(1)}, u32[]{:S(2)}) copy-start(f32[4,128,256]{2,1,0:T(8,128)S(1)} %collective-permute-done.1.refs_2_.refs_5_) | copy-start | bytes 1572868
  85.3 162.2 %copy-start.18 = (f32[4,128,256]{2,1,0:T(8,128)}, f32[4,128,256]{2,1,0:T(8,128)S(1)}, u32[]{:S(2)}) copy-start(f32[4,128,256]{2,1,0:T(8,128)S(1)} %collective-permute-done.refs_0_.refs_3_) | copy-start | bytes 1572868
  120.0 56.8 %all-to-all-start.2 = ((f32[256,16,128]{2,1,0:T(8,128)}), f32[256,16,128]{2,1,0:T(8,128)S(1)}, u32[]{:S(2)}, u32[]{:S(2)}) async-start(f32[256,16,128]{2,1,0:T(8,128)} %bitcast.114), calls=%async_computation.2 | async-start | bytes 4194304 | tf_op jit(solution)/shard_map/all_to_all | solution.py:275
  132.1 13.0 %collective-permute-start.3 = (f32[4,128,256]{2,1,0:T(8,128)}, f32[4,128,256]{2,1,0:T(8,128)S(1)}, u32[]{:S(2)}, u32[]{:S(2)}) collective-permute-start(f32[4,128,256]{2,1,0:T(8,128)} %get-tuple-element.45), channel_id=1, source_target_pairs={{1,0},{2,1},{3,2},{4,3},{5,4},{6,5},{7,6},{9,8},{10,9},{11,10},{12... | collective-permute-start | bytes 1572872 | tf_op jit(solution)/shard_map/ppermute | solution.py:258
  133.4 12.5 %collective-permute-start.2 = (f32[4,128,256]{2,1,0:T(8,128)}, f32[4,128,256]{2,1,0:T(8,128)}, u32[]{:S(2)}, u32[]{:S(2)}) collective-permute-start(f32[4,128,256]{2,1,0:T(8,128)} %get-tuple-element.46), channel_id=1, source_target_pairs={{0,1},{1,2},{2,3},{3,4},{4,5},{5,6},{6,7},{8,9},{9,10},{10,11},{11... | collective-permute-start | bytes 1572872 | tf_op jit(solution)/shard_map/ppermute | solution.py:258
  145.9 39.7 %copy-start.28 = (s32[1,8]{1,0:T(1,128)S(1)}, s32[1,8]{1,0:T(1,128)}, u32[]{:S(2)}) copy-start(s32[1,8]{1,0:T(1,128)} %param.9) | copy-start | bytes 100
  145.9 39.7 %copy-start.25 = (s32[1,8,1024]{2,1,0:T(8,128)S(1)}, s32[1,8,1024]{2,1,0:T(8,128)}, u32[]{:S(2)}) copy-start(s32[1,8,1024]{2,1,0:T(8,128)} %param.7) | copy-start | bytes 98308
  145.9 39.8 %copy-start.26 = (f32[1,8,1024]{2,1,0:T(8,128)S(1)}, f32[1,8,1024]{2,1,0:T(8,128)}, u32[]{:S(2)}) copy-start(f32[1,8,1024]{2,1,0:T(8,128)} %param.10) | copy-start | bytes 98308
  145.9 39.8 %copy-start.27 = (f32[1,8,1024]{2,1,0:T(8,128)S(1)}, f32[1,8,1024]{2,1,0:T(8,128)}, u32[]{:S(2)}) copy-start(f32[1,8,1024]{2,1,0:T(8,128)} %param.11) | copy-start | bytes 98308
  145.9 39.8 %copy-start.29 = (s32[1,8]{1,0:T(1,128)S(1)}, s32[1,8]{1,0:T(1,128)}, u32[]{:S(2)}) copy-start(s32[1,8]{1,0:T(1,128)} %param.8) | copy-start | bytes 100
  178.2 57.4 %all-to-all-start.3 = ((f32[256,16,128]{2,1,0:T(8,128)}), f32[256,16,128]{2,1,0:T(8,128)S(1)}, u32[]{:S(2)}, u32[]{:S(2)}) async-start(f32[256,16,128]{2,1,0:T(8,128)} %bitcast.113), calls=%async_computation.3 | async-start | bytes 4194304 | tf_op jit(solution)/shard_map/all_to_all | solution.py:275
  194.2 26.1 %collective-permute-start.5 = (f32[4,128,256]{2,1,0:T(8,128)}, f32[4,128,256]{2,1,0:T(8,128)}, u32[]{:S(2)}, u32[]{:S(2)}) collective-permute-start(f32[4,128,256]{2,1,0:T(8,128)} %get-tuple-element.43), channel_id=1, source_target_pairs={{1,0},{2,1},{3,2},{4,3},{5,4},{6,5},{7,6},{9,8},{10,9},{11,10},{12... | collective-permute-start | bytes 1572872 | tf_op jit(solution)/shard_map/ppermute | solution.py:258
  195.5 24.8 %collective-permute-start.4 = (f32[4,128,256]{2,1,0:T(8,128)}, f32[4,128,256]{2,1,0:T(8,128)}, u32[]{:S(2)}, u32[]{:S(2)}) collective-permute-start(f32[4,128,256]{2,1,0:T(8,128)} %get-tuple-element.44), channel_id=1, source_target_pairs={{0,1},{1,2},{2,3},{3,4},{4,5},{5,6},{6,7},{8,9},{9,10},{10,11},{11... | collective-permute-start | bytes 1572872 | tf_op jit(solution)/shard_map/ppermute | solution.py:258
  235.7 57.2 %all-to-all-start.4 = ((f32[256,16,128]{2,1,0:T(8,128)}), f32[256,16,128]{2,1,0:T(8,128)}, u32[]{:S(2)}, u32[]{:S(2)}) async-start(f32[256,16,128]{2,1,0:T(8,128)} %bitcast.117), calls=%async_computation.4 | async-start | bytes 4194304 | tf_op jit(solution)/shard_map/all_to_all | solution.py:275
  248.3 31.0 %collective-permute-start.8 = (f32[24,16,256]{2,1,0:T(8,128)}, f32[24,16,256]{2,1,0:T(8,128)}, u32[]{:S(2)}, u32[]{:S(2)}) collective-permute-start(f32[24,16,256]{2,1,0:T(8,128)} %pad_maximum_fusion), channel_id=1, source_target_pairs={{0,24},{8,0},{16,8},{24,16},{1,25},{9,1},{17,9},{25,17},{2,26},{10... | collective-permute-start | bytes 1179656 | tf_op jit(solution)/shard_map/ppermute | solution.py:258
  255.0 24.3 %collective-permute-start.7 = (f32[4,128,256]{2,1,0:T(8,128)}, f32[4,128,256]{2,1,0:T(8,128)S(1)}, u32[]{:S(2)}, u32[]{:S(2)}) collective-permute-start(f32[4,128,256]{2,1,0:T(8,128)} %get-tuple-element.41), channel_id=1, source_target_pairs={{1,0},{2,1},{3,2},{4,3},{5,4},{6,5},{7,6},{9,8},{10,9},{11,10},{12... | collective-permute-start | bytes 1572872 | tf_op jit(solution)/shard_map/ppermute | solution.py:258
  256.3 23.0 %collective-permute-start.6 = (f32[4,128,256]{2,1,0:T(8,128)}, f32[4,128,256]{2,1,0:T(8,128)S(1)}, u32[]{:S(2)}, u32[]{:S(2)}) collective-permute-start(f32[4,128,256]{2,1,0:T(8,128)} %get-tuple-element.42), channel_id=1, source_target_pairs={{0,1},{1,2},{2,3},{3,4},{4,5},{5,6},{6,7},{8,9},{9,10},{10,11},{11... | collective-permute-start | bytes 1572872 | tf_op jit(solution)/shard_map/ppermute | solution.py:258
  292.9 56.9 %all-to-all-start.5 = ((f32[256,16,128]{2,1,0:T(8,128)}), f32[256,16,128]{2,1,0:T(8,128)S(1)}, u32[]{:S(2)}, u32[]{:S(2)}) async-start(f32[256,16,128]{2,1,0:T(8,128)} %bitcast.118), calls=%async_computation.5 | async-start | bytes 4194304 | tf_op jit(solution)/shard_map/all_to_all | solution.py:275
  310.2 20.4 %collective-permute-start.9 = (f32[24,16,256]{2,1,0:T(8,128)S(1)}, f32[24,16,256]{2,1,0:T(8,128)}, u32[]{:S(2)}, u32[]{:S(2)}) collective-permute-start(f32[24,16,256]{2,1,0:T(8,128)S(1)} %pad_maximum_fusion.1), channel_id=1, source_target_pairs={{0,8},{8,16},{16,24},{24,0},{1,9},{9,17},{17,25},{25,1},{2,10},{10... | collective-permute-start | bytes 1179656 | tf_op jit(solution)/shard_map/ppermute | solution.py:258
  349.8 53.6 %all-to-all-start.6 = ((f32[256,16,128]{2,1,0:T(8,128)}), f32[256,16,128]{2,1,0:T(8,128)}, u32[]{:S(2)}, u32[]{:S(2)}) async-start(f32[256,16,128]{2,1,0:T(8,128)} %copy.46), calls=%async_computation.6 | async-start | bytes 4194304 | tf_op jit(solution)/shard_map/all_to_all | solution.py:275
  (23 other events, 62.9 us)
